TPU v7x, 128 devices: a whole 4x4x4 slice. The times are simulated.
128 devices in a mesh: group: 2 (over core), ctx: 32 (over y_hi, z, x), mp: 2 (over y_lo).
Axes of the slice: x: 4, y: 4 (y_hi: 2, y_lo: 2; y = y_hi * 2 + y_lo), z: 4, core: 2. Of those that a mesh axis runs over, the one named last changes fastest.
Arguments:
- token_ids: int32 [2, 4096], P('group', 'ctx'), may hold values from 0 to 127
- span_offset: int32 [1], replicated, may hold values from 0 to 12287
- shard_lengths: int32 [32], P('ctx'), may hold values from 1 to 384
- embed_table: bfloat16 [128, 2560], P(None, 'mp'), may hold values from -6 to 6
- norm_gain: bfloat16 [2560], P('mp'), may hold values from 0.25 to 1.75
- query_weight: bfloat16 [2560, 2560], P('mp'), may hold values from -0.25 to 0.25
- key_weight: bfloat16 [2560, 2560], P('mp'), may hold values from -0.25 to 0.25
- value_weight: bfloat16 [2560, 2560], P('mp'), may hold values from -0.125 to 0.125
- cache_keys: bfloat16 [12288, 2560], P('ctx', 'mp'), may hold values from -440 to 440
- cache_values: bfloat16 [12288, 2560], P('ctx', 'mp'), may hold values from -6 to 6
Outputs:
- attended: bfloat16 [2, 4096, 2560], P('group', 'ctx', 'mp')
All inputs are finite; a program needn't handle non-finite values.
Results may differ from a plain program's by a relative error of at most 0.012.
The roundings to bfloat16 on the way count: a program that leaves them out, or rounds other values in their place, can miss the bound.
Values may be sent and summed in bfloat16 or wider, within the bound.
No kernel may reach another device: no remote copies, remote signals or barrier semaphores. Data moves between devices by JAX's collectives and lax.ppermute only.
A program may use at most 256 MiB of HBM per device.

v0:
```python
import math

import jax
import jax.numpy as jnp
from jax import lax
from jax.sharding import PartitionSpec as P

D = 2560
HD = 80
PROT = 256
STEPS = 4


def passed_along(value, axis, steps):
    count = lax.axis_size(axis)
    first, last = (max(0, -steps), min(count, count - steps))
    return lax.ppermute(value, axis, [(source, source + steps) for source in range(first, last)])


def rotate(values_in, positions):
    row_count = values_in.shape[0]
    head_count = values_in.shape[1] // HD
    quarter = HD // 4
    column = (positions % PROT).astype(jnp.float32)
    homolog = (positions // PROT).astype(jnp.float32)
    frequency = 10000.0 ** (-jnp.arange(quarter, dtype=jnp.float32) / quarter)
    angles = jnp.stack([column[:, None] * frequency, homolog[:, None] * frequency], 1)
    cosine = jnp.cos(angles)[:, None, :, None, :]
    sine_table = jnp.sin(angles)[:, None, :, None, :]
    pieces = values_in.reshape(row_count, head_count, 2, 2, quarter)
    partner = jnp.stack([-pieces[:, :, :, 1], pieces[:, :, :, 0]], 3)
    return (pieces * cosine + partner * sine_table).reshape(row_count, head_count * HD)


def block_partial(
    query_block, start, all_keys, all_values, live_length, span_base, cache_count, decoding
):
    block_rows = query_block.shape[0]
    head_count = query_block.shape[1] // HD
    key_slots = all_keys.shape[0]
    query_heads = query_block.reshape(block_rows, head_count, HD)
    key_heads = all_keys.reshape(key_slots, head_count, HD)
    value_heads = all_values.reshape(key_slots, head_count, HD)
    scores = jnp.einsum(
        "qhd,khd->hqk", query_heads, key_heads, preferred_element_type=jnp.float32
    ) * (1.0 / math.sqrt(HD))
    slot = jnp.arange(key_slots, dtype=jnp.int32)
    query_index = start + jnp.arange(block_rows, dtype=jnp.int32)
    cache_live = (slot < cache_count) & (slot < live_length)
    span_index = span_base + slot - cache_count
    span_seen = (slot >= cache_count)[None, :] & (
        decoding | (span_index[None, :] <= query_index[:, None])
    )
    visible = (cache_live[None, :] | span_seen)[None]
    block_max = jnp.max(jnp.where(visible, scores, -1e30), -1)
    weights = jnp.where(visible, jnp.exp(scores - block_max[..., None]), 0.0)
    block_sum = jnp.sum(weights, -1)
    block_acc = jnp.einsum(
        "hqk,khd->qhd",
        weights.astype(jnp.bfloat16),
        value_heads,
        preferred_element_type=jnp.float32,
    )
    return (block_max.T, block_sum.T, block_acc.reshape(block_rows, head_count * HD))


def local(
    token_ids,
    span_offset,
    shard_lengths,
    embed_table,
    norm_gain,
    query_weight,
    key_weight,
    value_weight,
    cache_keys,
    cache_values,
):
    token_row = token_ids[0]
    row_count = token_row.shape[0]
    ctx_count = lax.axis_size("ctx")
    ctx_index = lax.axis_index("ctx")
    decoding = lax.axis_index("group") == 1
    one_hot = (
        token_row[:, None] == jnp.arange(embed_table.shape[0], dtype=jnp.int32)[None, :]
    ).astype(jnp.bfloat16)
    embedded = jnp.dot(one_hot, embed_table, preferred_element_type=jnp.float32)
    square_sum = lax.psum(jnp.sum(embedded * embedded, 1), "mp")
    normal_rows = (
        embedded * lax.rsqrt(square_sum / D + 1e-05)[:, None] * norm_gain.astype(jnp.float32)
    ).astype(jnp.bfloat16)
    query_part = jnp.dot(normal_rows, query_weight, preferred_element_type=jnp.float32)
    key_part = jnp.dot(normal_rows, key_weight, preferred_element_type=jnp.float32)
    value_part = jnp.dot(normal_rows, value_weight, preferred_element_type=jnp.float32)
    query_full, key_full, value_full = (
        lax.psum_scatter(query_part, "mp", scatter_dimension=1, tiled=True),
        lax.psum_scatter(key_part, "mp", scatter_dimension=1, tiled=True),
        lax.psum_scatter(value_part, "mp", scatter_dimension=1, tiled=True),
    )
    offset_value = span_offset[0]
    local_iota = jnp.arange(row_count, dtype=jnp.int32)
    positions = jnp.where(
        decoding,
        offset_value + row_count * ctx_count + local_iota % STEPS,
        offset_value + ctx_index * row_count + local_iota,
    )
    queries = rotate(query_full, positions).astype(jnp.bfloat16)
    new_keys = rotate(key_full, positions).astype(jnp.bfloat16)
    new_values = value_full.astype(jnp.bfloat16)
    width = queries.shape[1]
    head_count = width // HD
    span_keys, span_values = passed_along((new_keys, new_values), "group", 1)
    block_keys = jnp.where(decoding, span_keys, new_keys)
    block_values = jnp.where(decoding, span_values, new_values)
    cache_count = cache_keys.shape[0]
    all_keys = jnp.concatenate([cache_keys, block_keys], 0)
    all_values = jnp.concatenate([cache_values, block_values], 0)
    live_length = shard_lengths[0]
    span_base = ctx_index * row_count
    gathered = lax.all_gather(queries, "ctx", axis=0, tiled=True)
    total = gathered.shape[0]
    block_rows = math.gcd(total, 512)
    block_count = total // block_rows
    block_starts = jnp.arange(block_count, dtype=jnp.int32) * block_rows

    def one_block(pair):
        return block_partial(
            pair[0], pair[1], all_keys, all_values, live_length, span_base, cache_count, decoding
        )

    maxima, totals, sums = lax.map(
        one_block, (gathered.reshape(block_count, block_rows, width), block_starts)
    )
    maxima = maxima.reshape(total, head_count)
    totals = totals.reshape(total, head_count)
    sums = sums.reshape(total, width)
    got_max, got_sum, got_acc = (
        lax.all_to_all(maxima[None], "ctx", split_axis=1, concat_axis=0, tiled=True),
        lax.all_to_all(totals[None], "ctx", split_axis=1, concat_axis=0, tiled=True),
        lax.all_to_all(sums[None], "ctx", split_axis=1, concat_axis=0, tiled=True),
    )
    whole_max = jnp.max(got_max, 0)
    rescale = jnp.exp(got_max - whole_max[None])
    whole_sum = jnp.sum(rescale * got_sum, 0)
    whole_acc = jnp.sum(got_acc * jnp.repeat(rescale, HD, axis=2), 0)
    cands = row_count // STEPS
    own_q = queries.reshape(cands, STEPS, head_count, HD)
    own_k = new_keys.reshape(cands, STEPS, head_count, HD)
    own_v = new_values.reshape(cands, STEPS, head_count, HD)
    own_scores = jnp.einsum("ashd,athd->ahst", own_q, own_k, preferred_element_type=jnp.float32) * (
        1.0 / math.sqrt(HD)
    )
    step_iota = jnp.arange(STEPS, dtype=jnp.int32)
    own_visible = (step_iota[None, :] <= step_iota[:, None]) & decoding
    own_max = jnp.max(jnp.where(own_visible, own_scores, -1e30), -1)
    final_max = jnp.maximum(whole_max, own_max.transpose(0, 2, 1).reshape(row_count, head_count))
    keep_old = jnp.exp(whole_max - final_max)
    final_cand = final_max.reshape(cands, STEPS, head_count).transpose(0, 2, 1)
    own_weights = jnp.where(own_visible, jnp.exp(own_scores - final_cand[..., None]), 0.0)
    own_sum = jnp.sum(own_weights, -1).transpose(0, 2, 1).reshape(row_count, head_count)
    own_acc = jnp.einsum(
        "ahst,athd->ashd",
        own_weights.astype(jnp.bfloat16),
        own_v,
        preferred_element_type=jnp.float32,
    ).reshape(row_count, width)
    numer = whole_acc * jnp.repeat(keep_old, HD, axis=1) + own_acc
    denom = whole_sum * keep_old + own_sum
    output = numer / jnp.repeat(denom, HD, axis=1)
    return output.astype(jnp.bfloat16)[None]


def solution(mesh):
    placed = (
        P("group", "ctx"),
        P(),
        P("ctx"),
        P(None, "mp"),
        P("mp"),
        P("mp", None),
        P("mp", None),
        P("mp", None),
        P("ctx", "mp"),
        P("ctx", "mp"),
    )
    return jax.shard_map(
        local, mesh=mesh, in_specs=placed, out_specs=P("group", "ctx", "mp"), check_vma=False
    )
```

profile of v0, /device:TPU:106, one launch (start us, length us, event | category | flops | bytes accessed | tf_op | source)
XLA Modules:
  0.0 992.7 jit_solution(8170254496922209624)
XLA Ops:
  8.5 4.9 psum.7
  13.6 5.0 fusion.29
  18.7 5.0 fusion.28
  23.7 4.9 fusion.30
  30.8 14.0 %reduce-scatter.6.cloned.1.call-done = f32[128,1280]{1,0:T(8,128)} async-done(((f32[128,2560]{1,0:T(8,128)}), f32[128,1280]{1,0:T(8,128)}) %reduce-scatter.6.cloned.1.call-update) | async-done | bytes 655376 | tf_op jit(solution)/shard_map/reduce_scatter | solution.py:97
  46.2 27.7 %reduce-scatter.4.cloned.1.call-done = f32[128,1280]{1,0:T(8,128)} async-done(((f32[128,2560]{1,0:T(8,128)}), f32[128,1280]{1,0:T(8,128)}) %reduce-scatter.4.cloned.1.call-update) | async-done | bytes 655376 | tf_op jit(solution)/shard_map/reduce_scatter | solution.py:96
  77.0 2.6 add_convert_fusion.1
  79.6 23.4 %reduce-scatter.8.cloned.1.call-done = f32[128,1280]{1,0:T(8,128)} async-done(((f32[128,2560]{1,0:T(8,128)}), f32[128,1280]{1,0:T(8,128)}) %reduce-scatter.8.cloned.1.call-update) | async-done | bytes 655376 | tf_op jit(solution)/shard_map/reduce_scatter | solution.py:98
  109.1 2.2 collective-permute-start
  115.3 106.0 %all-gather.2.cloned.1.call-done = bf16[4096,1280]{1,0:T(8,128)(2,1)} async-done(((bf16[128,1280]{1,0:T(8,128)(2,1)}), bf16[4096,1280]{1,0:T(8,128)(2,1)}) %all-gather.2.cloned.1.call-update) | async-done | bytes 10485776 | tf_op jit(solution)/shard_map/all_gather | solution.py:120
  221.3 288.1 %while.16 = (s32[]{:T(128)}, f32[8,512,16]{1,2,0:T(8,128)S(1)}, f32[8,512,16]{1,2,0:T(8,128)}, f32[8,512,1280]{2,1,0:T(8,128)}, s32[]{:T(128)}, /*index=5*/pred[...) while((s32[]{:T(128)}, f32[8,512,16]{1,2,0:T(8,128)S(1)}, ...), condition=%wide.region_8.9_spmd, body=%wide.region_5.8_spmd.sunk | while | flops 1389350400 | bytes 79177912 | solution.py:131
  225.7 8.8 select_reduce_fusion.3
  234.5 9.3 fusion.54
  243.8 9.1 fusion.55
  252.9 2.1 copy.222
  255.7 1.7 constant_dynamic-update-slice_fusion.2
  261.8 8.8 select_reduce_fusion.3
  270.6 9.3 fusion.54
  279.8 9.1 fusion.55
  288.9 2.1 copy.222
  291.7 1.7 constant_dynamic-update-slice_fusion.2
  297.8 8.8 select_reduce_fusion.3
  306.6 9.3 fusion.54
  315.9 9.1 fusion.55
  325.0 2.1 copy.222
  327.7 1.6 constant_dynamic-update-slice_fusion.2
  333.8 8.8 select_reduce_fusion.3
  342.6 9.3 fusion.54
  351.9 9.1 fusion.55
  361.0 2.1 copy.222
  363.7 1.7 constant_dynamic-update-slice_fusion.2
  369.9 8.8 select_reduce_fusion.3
  378.7 9.3 fusion.54
  387.9 9.1 fusion.55
  397.0 2.1 copy.222
  405.9 8.8 select_reduce_fusion.3
  414.7 9.3 fusion.54
  423.9 9.1 fusion.55
  433.0 2.1 copy.222
  441.9 8.8 select_reduce_fusion.3
  450.6 9.3 fusion.54
  459.9 9.1 fusion.55
  469.0 2.1 copy.222
  477.8 8.8 select_reduce_fusion.3
  486.6 9.3 fusion.54
  495.9 9.1 fusion.55
  505.0 2.1 copy.222
  510.5 19.6 %reduce = f32[4096,16]{1,0:T(8,128)} reduce(f32[4096,1,16]{2,1,0:T(1,128)S(1)} %bitcast.105, f32[]{:T(128)} %broadcast.347), dimensions={1}, to_apply=%bitcast.62.reduce_sub_computation | reduce | bytes 524292
  530.1 3.0 reshape.390
  533.1 7.9 all-to-all-start.1
  541.6 19.4 %reduce.2 = f32[4096,16]{1,0:T(8,128)} reduce(f32[4096,1,16]{2,1,0:T(1,128)S(1)} %bitcast.106, f32[]{:T(128)} %broadcast.347), dimensions={1}, to_apply=%bitcast.64.reduce_sub_computation | reduce | bytes 524292
  561.0 3.0 reshape.392
  564.0 9.8 all-to-all-start.2
  573.8 24.6 %copy.168 = f32[1,4096,1280]{2,0,1:T(1,128)} copy(f32[1,4096,1280]{2,1,0:T(8,128)} %bitcast.101) | data formatting | bytes 41943040 | tf_op jit(solution)/shard_map/broadcast_in_dim;reshape | solution.py:140
  599.1 10.3 %all-to-all-start = ((f32[1,4096,1280]{2,0,1:T(1,128)}), f32[1,4096,1280]{2,0,1:T(1,128)}, u32[]{:S(2)}, u32[]{:S(2)}) async-start(f32[1,4096,1280]{2,0,1:T(1,128)} %copy.168), calls=%async_computation.3 | async-start | bytes 41943040 | tf_op jit(solution)/shard_map/all_to_all | solution.py:140
  615.7 3.9 reshape.391
  624.5 2.2 reduce.3
  626.7 4.1 reshape.393
  632.3 8.4 broadcast_in_dim.99
  640.7 22.6 %copy.174 = f32[32,128,1280]{2,1,0:T(8,128)} copy(f32[32,128,1280]{1,2,0:T(8,128)} %bitcast.99) | data formatting | bytes 41943040 | tf_op jit(solution)/shard_map/reshape | solution.py:145
  663.3 292.7 %all-to-all-done = f32[1,4096,1280]{2,0,1:T(1,128)} async-done(((f32[1,4096,1280]{2,0,1:T(1,128)}), f32[1,4096,1280]{2,0,1:T(1,128)}, u32[]{:S(2)}, u32[]{:S(2)}) %all-to-all-start) | async-done | bytes 20971552 | tf_op jit(solution)/shard_map/all_to_all | solution.py:140
  956.0 18.5 %copy.203 = f32[1,4096,1280]{2,1,0:T(8,128)} copy(f32[1,4096,1280]{2,0,1:T(1,128)} %all-to-all-done) | data formatting | bytes 41943040
  974.5 1.8 copy-done.2
  976.3 8.7 multiply_reduce_fusion
  (190 shorter events, 80.4 us)
Async XLA Ops:
  6.5 1.0 copy-start
  6.5 38.3 %reduce-scatter.6.cloned.1.call-start = ((), (), s32[]{:S(2)}) async-start(), calls=%async_computation.8 | async-start | bytes 1966080 | tf_op jit(solution)/shard_map/reduce_scatter | solution.py:97
  18.6 55.3 %reduce-scatter.4.cloned.1.call-start = ((), (), s32[]{:S(2)}) async-start(), calls=%async_computation.6 | async-start | bytes 1966080 | tf_op jit(solution)/shard_map/reduce_scatter | solution.py:96
  23.7 79.4 %reduce-scatter.8.cloned.1.call-start = ((), (), s32[]{:S(2)}) async-start(), calls=%async_computation.9 | async-start | bytes 1966080 | tf_op jit(solution)/shard_map/reduce_scatter | solution.py:98
  28.7 192.6 %all-gather.2.cloned.1.call-start = ((), (), s32[]{:S(2)}) async-start(), calls=%async_computation.7 | async-start | bytes 10813440 | tf_op jit(solution)/shard_map/all_gather | solution.py:120
  104.2 7.0 copy-start.5
  104.2 7.0 collective-permute-start.1
  109.1 3.6 collective-permute-start
  234.5 9.3 copy-start.4
  270.6 9.3 copy-start.4
  306.6 9.3 copy-start.4
  342.6 9.3 copy-start.4
  378.7 9.3 copy-start.4
  414.7 9.3 copy-start.4
  450.6 9.3 copy-start.4
  486.6 9.3 copy-start.4
  509.4 31.6 %copy-start.8 = (f32[8,512,16]{1,2,0:T(8,128)S(1)}, f32[8,512,16]{1,2,0:T(8,128)}, u32[]{:S(2)}) copy-start(f32[8,512,16]{1,2,0:T(8,128)} %get-tuple-element.146) | copy-start | bytes 786436
  533.1 30.9 %all-to-all-start.1 = ((f32[32,1,2048]{2,1,0:T(1,128)}), f32[32,1,2048]{2,1,0:T(1,128)S(1)}, u32[]{:S(2)}, u32[]{:S(2)}) async-start(f32[32,1,2048]{2,1,0:T(1,128)} %reshape.390), calls=%async_computation.4 | async-start | bytes 524288 | tf_op jit(solution)/shard_map/all_to_all | solution.py:138
  564.0 34.4 %all-to-all-start.2 = ((f32[32,1,2048]{2,1,0:T(1,128)}), f32[32,1,2048]{2,1,0:T(1,128)S(1)}, u32[]{:S(2)}, u32[]{:S(2)}) async-start(f32[32,1,2048]{2,1,0:T(1,128)} %reshape.392), calls=%async_computation.5 | async-start | bytes 524288 | tf_op jit(solution)/shard_map/all_to_all | solution.py:139
  598.4 11.0 %copy-start.6 = (bf16[128,1280]{1,0:T(8,128)(2,1)S(1)}, bf16[128,1280]{1,0:T(8,128)(2,1)}, u32[]{:S(2)}) copy-start(bf16[128,1280]{1,0:T(8,128)(2,1)} %copy-done.5) | copy-start | bytes 983044
  598.4 12.6 %copy-start.3 = (bf16[128,1280]{1,0:T(8,128)(2,1)S(1)}, bf16[128,1280]{1,0:T(8,128)(2,1)}, u32[]{:S(2)}) copy-start(bf16[128,1280]{1,0:T(8,128)(2,1)} %get-tuple-element.247) | copy-start | bytes 983044
  598.4 0.7 copy-start.7
  599.1 356.8 %all-to-all-start = ((f32[1,4096,1280]{2,0,1:T(1,128)}), f32[1,4096,1280]{2,0,1:T(1,128)}, u32[]{:S(2)}, u32[]{:S(2)}) async-start(f32[1,4096,1280]{2,0,1:T(1,128)} %copy.168), calls=%async_computation.3 | async-start | bytes 41943040 | tf_op jit(solution)/shard_map/all_to_all | solution.py:140
  956.0 20.3 %copy-start.2 = (f32[32,128,1280]{2,1,0:T(8,128)S(1)}, f32[32,128,1280]{2,1,0:T(8,128)}, u32[]{:S(2)}) copy-start(f32[32,128,1280]{2,1,0:T(8,128)} %copy.174) | copy-start | bytes 62914564
  976.3 9.6 copy-start.1
Sparse Core Ops, SparseCore 0:
  18.7 26.0 reduce-scatter.5
  47.2 26.7 reduce-scatter.3
  76.3 26.7 reduce-scatter.7
  106.0 115.2 all-gather.1
where the time goes:
time: 1000 us; the launch traced here: 993 us
  waiting for transfers between devices  464 us (46%)
  local copies, waits for them, and re-layouts  167 us (17%)
  matrix products  160 us (16%)
  other arithmetic  149 us (15%)
  starting transfers between devices  32 us (3%)
  between operations  14.5 us (1%)
    all_to_all x1, waiting for transfers between devices, local(): lax.all_to_all(sums[None], 'ctx', split_axis=1, concat_axis=0, tiled=True)  293 us
    all_gather x1, waiting for transfers between devices, local(): gathered = lax.all_gather(queries, 'ctx', axis=0, tiled=True)  106 us
    reduce_sum x8, other arithmetic, block_partial(): block_sum = jnp.sum(weights, -1)  74 us
    dot_general x8, matrix products, block_partial(): jnp.einsum('hqk,khd->qhd', weights.astype(jnp.bfloat16), value_heads, pre...  72.7 us
    dot_general x8, matrix products, block_partial(): jnp.einsum('qhd,khd->hqk', query_heads, key_heads, preferred_element_type...  70.2 us
    unnamed x26, local copies, waits for them, and re-layouts  39.9 us
    unnamed x2, other arithmetic  38.9 us
    dynamic_update_slice x24, local copies, waits for them, and re-layouts, local(): lax.map(one_block, (gathered.reshape(block_count, block_rows, width), blo...  35.4 us
  transfers between devices with their start and end apart: 9, of which 5 were waited for; matrix products, arithmetic and copies ran while one was open for 13% of the time, Pallas kernels for 0%

commit v1 on v0

v1 whole, which is shorter than its diff:
```python
import math

import jax
import jax.numpy as jnp
from jax import lax
from jax.experimental import pallas as pl
from jax.experimental.pallas import tpu as pltpu
from jax.sharding import Mesh
from jax.sharding import PartitionSpec as P

D = 2560
HALF = 1280
HD = 80
PROT = 256
STEPS = 4
VOCAB = 128
PLANE = 16
N_CTX = 32
ROWS = 128
CACHE = 384
TILE = 256
SLOTS = 10
SENT = 6
GS = 2
KB = 1024
KB_NEW = 512
SCALE2 = math.log2(math.e) / math.sqrt(HD)
LOW = -1e30
DEAD = -2e30
F32 = jnp.float32
BF16 = jnp.bfloat16
TILES = ((0, 1, 2, 3, 10, 11, 12, 13, 14, 15), (4, 5, 6, 7, 8, 9, 16, 17, 0, 0))


def vm():
    return pl.BlockSpec(memory_space=pltpu.MemorySpace.VMEM)


def sm():
    return pl.BlockSpec(memory_space=pltpu.MemorySpace.SMEM)


def anyspace():
    return pl.BlockSpec(memory_space=pl.ANY)


def params():
    return pltpu.CompilerParams(vmem_limit_bytes=56 << 20)


def split3(x):
    high = x.astype(BF16)
    rest = x - high.astype(F32)
    mid = rest.astype(BF16)
    low = (rest - mid.astype(F32)).astype(BF16)
    return high, mid, low


def first_row(shape, value):
    return jnp.where(lax.broadcasted_iota(jnp.int32, shape, 0) == 0, value, 0.0)


def turn_kernel(where_ref, keys_ref, values_ref, out_ref, buf, sem):
    @pl.when(where_ref[0] == 0)
    def _():
        pltpu.make_async_copy(keys_ref, buf, sem).start()

    @pl.when(where_ref[0] != 0)
    def _():
        pltpu.make_async_copy(values_ref, buf, sem).start()

    pltpu.make_async_copy(keys_ref, buf, sem).wait()
    for block in range(HALF // 128):
        out_ref[block * 128 : block * 128 + 128, :] = buf[:, block * 128 : block * 128 + 128].T


def turn(where, keys, values):
    return pl.pallas_call(
        turn_kernel,
        out_shape=jax.ShapeDtypeStruct((HALF, CACHE), BF16),
        in_specs=[sm(), anyspace(), anyspace()],
        out_specs=vm(),
        scratch_shapes=[pltpu.VMEM((CACHE, HALF), BF16), pltpu.SemaphoreType.DMA(())],
        compiler_params=params(),
        name="turn",
    )(where, keys, values)


def table_kernel(where_ref, embed_ref, gain_ref, square_ref, wq, wk, wv, own_ref, other_ref, buf, turned, sems):
    mp = where_ref[2]
    head = where_ref[3]
    base = jnp.minimum((head * HD) // 128 * 128, 1024)
    inside = pl.multiple_of(head * HD - base, 16)
    halves = (mp, 1 - mp)
    for half in range(2):
        at = pl.multiple_of(halves[half] * HALF + base, 128)
        for which, weight in enumerate((wq, wk, wv)):
            pltpu.make_async_copy(
                weight.at[:, pl.ds(at, 256)], buf.at[half * 3 + which], sems.at[half * 3 + which]
            ).start()
    mean = square_ref[...] / D
    normal = (
        embed_ref[...].astype(F32) * lax.rsqrt(mean + 1e-05) * gain_ref[...].astype(F32)
    ).astype(BF16)
    for half in (1, 0):
        for which in range(3):
            pltpu.make_async_copy(
                wq.at[:, pl.ds(0, 256)], buf.at[half * 3 + which], sems.at[half * 3 + which]
            ).wait()
            turned[...] = jnp.dot(normal, buf[half * 3 + which], preferred_element_type=F32).T
            out = own_ref if half == 0 else other_ref
            out[which * HD : which * HD + HD, :] = turned[pl.ds(inside, HD), :]


def table(where, embed, gain, square, wq, wk, wv):
    return pl.pallas_call(
        table_kernel,
        out_shape=[jax.ShapeDtypeStruct((3 * HD, VOCAB), F32)] * 2,
        in_specs=[sm(), vm(), vm(), vm(), anyspace(), anyspace(), anyspace()],
        out_specs=[vm(), vm()],
        scratch_shapes=[
            pltpu.VMEM((6, HALF, 256), BF16),
            pltpu.VMEM((256, VOCAB), F32),
            pltpu.SemaphoreType.DMA((6,)),
        ],
        compiler_params=params(),
        name="table",
    )(where, embed, gain, square, wq, wk, wv)


def flash_step(queries, keys, values, state_max, state_acc, limit=None, key_index=None):
    scores = jnp.dot(keys, queries, preferred_element_type=F32)
    if limit is not None:
        scores = jnp.where(key_index <= limit, scores, DEAD)
    new_max = jnp.maximum(state_max, jnp.max(scores, 0, keepdims=True))
    weights = jnp.exp2(scores - new_max).astype(BF16)
    acc = state_acc * jnp.exp2(state_max - new_max) + jnp.dot(
        values, weights, preferred_element_type=F32
    )
    return new_max, acc


def fresh_kernel(
    where_ref,
    own_ref,
    recv_ref,
    ids_ref,
    dec_ref,
    cos_ref,
    sin_ref,
    query_ref,
    max_ref,
    acc_ref,
    own_out,
    keys,
    values,
    wide,
):
    group = where_ref[0]
    plane = where_ref[1]
    quarter = HD // 4
    tables = own_ref[...] + recv_ref[...]
    row = lax.broadcasted_iota(jnp.int32, (HD, VOCAB), 0)
    upper = (row // quarter) % 2 == 0

    def stacked(part):
        partner = jnp.where(
            upper, -pltpu.roll(part, HD - quarter, 0), pltpu.roll(part, quarter, 0)
        )
        pieces = []
        for item in (part, partner):
            high = item.astype(BF16)
            pieces += [high, (item - high.astype(F32)).astype(BF16)]
        return jnp.concatenate(pieces, 0)

    query_table = stacked(tables[0:HD])
    key_table = stacked(tables[HD : 2 * HD])
    value_table = tables[2 * HD :].astype(BF16)
    tail_keys = jnp.zeros((16, TILE), BF16)
    ones_row = first_row((16, TILE), 1.0).astype(BF16)

    def chosen(tile):
        return (
            lax.broadcasted_iota(jnp.int32, (VOCAB, TILE), 0) == ids_ref[tile]
        ).astype(BF16)

    def turned_by(one_hot, stack, tile):
        raw = jnp.dot(stack, one_hot, preferred_element_type=F32)
        plain = raw[0:HD] + raw[HD : 2 * HD]
        partner = raw[2 * HD : 3 * HD] + raw[3 * HD :]
        return (plain * cos_ref[tile] + partner * sin_ref[tile]).astype(BF16)

    def tile_of(slot):
        return where_ref[4 + slot]

    def one_query(slot, carry):
        tile = tile_of(slot)
        rotated = turned_by(chosen(tile), query_table, tile)
        query_ref[slot] = jnp.concatenate([*split3(rotated.astype(F32) * SCALE2), ones_row], 0)
        return carry

    lax.fori_loop(0, SLOTS, one_query, 0, unroll=2)

    def one_key(block, carry):
        tile = 2 * block + plane
        one_hot = chosen(tile)
        rotated = turned_by(one_hot, key_table, tile)
        keys[block] = jnp.concatenate([rotated, rotated, rotated, tail_keys], 0).T
        picked = jnp.dot(value_table, one_hot, preferred_element_type=F32).astype(BF16)
        values[block] = jnp.concatenate([picked, ones_row], 0)
        return carry

    lax.fori_loop(0, 8, one_key, 0, unroll=2)

    for first in range(0, SLOTS, GS):
        last_tile = tile_of(first + GS - 1)
        most = jnp.where(last_tile >= PLANE, 8, (last_tile - plane) // 2 + 1)
        most = jnp.where((first >= 8) & (group == 1), 0, most)
        chunks = (most + 1) // 2
        for slot in range(first, first + GS):
            max_ref[slot] = jnp.full((1, TILE), LOW, F32)
            acc_ref[slot] = jnp.zeros((96, TILE), F32)

        def chunk(step, carry, first=first):
            key_part = jnp.concatenate([keys[2 * step], keys[2 * step + 1]], 0)
            value_part = jnp.concatenate([values[2 * step], values[2 * step + 1]], 1)
            row_at = lax.broadcasted_iota(jnp.int32, (KB_NEW, TILE), 0)
            key_index = row_at + jnp.where(row_at >= TILE, TILE, 0) + (4 * step + plane) * TILE
            lane = lax.broadcasted_iota(jnp.int32, (1, TILE), 1)
            for slot in range(first, first + GS):
                tile = tile_of(slot)
                limit = jnp.where(tile >= PLANE, 1 << 20, tile * TILE) + lane
                max_ref[slot], acc_ref[slot] = flash_step(
                    query_ref[slot],
                    key_part,
                    value_part,
                    max_ref[slot],
                    acc_ref[slot],
                    limit,
                    key_index,
                )
            return carry

        lax.fori_loop(0, chunks, chunk, 0)

    @pl.when(group == 1)
    def _():
        for part in range(2):
            lanes = slice(part * TILE, part * TILE + TILE)
            one_hot = chosen(16 + part)
            wide[0 : 3 * HD, lanes] = query_ref[SENT + part, 0 : 3 * HD, :]
            wide[3 * HD : 4 * HD, lanes] = turned_by(one_hot, key_table, 16 + part)
            wide[4 * HD : 5 * HD, lanes] = jnp.dot(
                value_table, one_hot, preferred_element_type=F32
            ).astype(BF16)
        key_at = lax.broadcasted_iota(jnp.int32, (ROWS, ROWS), 0)
        query_at = lax.broadcasted_iota(jnp.int32, (ROWS, ROWS), 1)
        seen = (key_at // STEPS == query_at // STEPS) & (key_at <= query_at)
        ones_tail = first_row((16, ROWS), 1.0).astype(BF16)
        zero_tail = jnp.zeros((16, ROWS), BF16)

        def one_block(item, carry):
            one_hot = decode_choice(dec_ref[plane * PLANE + item])
            picked = jnp.dot(wide[...], one_hot, preferred_element_type=F32).astype(BF16)
            queries = jnp.concatenate([picked[0 : 3 * HD], ones_tail], 0)
            own_keys = picked[3 * HD : 4 * HD]
            own_keys = jnp.concatenate([own_keys, own_keys, own_keys, zero_tail], 0).T
            scores = jnp.dot(own_keys, queries, preferred_element_type=F32)
            scores = jnp.where(seen, scores, DEAD)
            top = jnp.max(scores, 0, keepdims=True)
            weights = jnp.exp2(scores - top).astype(BF16)
            acc = jnp.dot(
                jnp.concatenate([picked[4 * HD :], ones_tail], 0),
                weights,
                preferred_element_type=F32,
            )
            total = acc[HD : HD + 1]
            own_out[item, 0:HD] = acc[0:HD] / total
            own_out[item, HD:88] = jnp.broadcast_to(top + jnp.log2(total), (8, ROWS))
            return carry

        lax.fori_loop(0, PLANE, one_block, 0, unroll=4)


def decode_choice(ids):
    lane = lax.broadcasted_iota(jnp.int32, (1, ROWS), 1)
    wanted = (lane % STEPS) * VOCAB + ids
    return (lax.broadcasted_iota(jnp.int32, (STEPS * VOCAB, ROWS), 0) == wanted).astype(BF16)


def fresh(where, own, recv, ids, dec, cosine, sine):
    return pl.pallas_call(
        fresh_kernel,
        out_shape=[
            jax.ShapeDtypeStruct((SLOTS, 256, TILE), BF16),
            jax.ShapeDtypeStruct((SLOTS, 1, TILE), F32),
            jax.ShapeDtypeStruct((SLOTS, 96, TILE), F32),
            jax.ShapeDtypeStruct((PLANE, 88, ROWS), F32),
        ],
        in_specs=[sm()] + [vm()] * 6,
        out_specs=[vm()] * 4,
        scratch_shapes=[
            pltpu.VMEM((8, TILE, 256), BF16),
            pltpu.VMEM((8, 96, TILE), BF16),
            pltpu.VMEM((5 * HD, STEPS * VOCAB), BF16),
        ],
        compiler_params=params(),
        name="fresh",
    )(where, own, recv, ids, dec, cosine, sine)


BLOCKS = PLANE * 3 + KB // 128 + 2


def cached_kernel(
    where_ref,
    length_ref,
    mine_ref,
    peer_ref,
    query_ref,
    max_in,
    acc_in,
    sent_ref,
    kept_ref,
    key_buf,
    value_buf,
    keys,
    values,
    max_ref,
    acc_ref,
    sems,
):
    group = where_ref[0]

    @pl.when(group == 0)
    def _():
        pltpu.make_async_copy(mine_ref, key_buf, sems.at[0]).start()
        pltpu.make_async_copy(peer_ref, value_buf, sems.at[1]).start()

    @pl.when(group != 0)
    def _():
        pltpu.make_async_copy(peer_ref, key_buf, sems.at[0]).start()
        pltpu.make_async_copy(mine_ref, value_buf, sems.at[1]).start()

    pltpu.make_async_copy(mine_ref, key_buf, sems.at[0]).wait()
    pltpu.make_async_copy(mine_ref, value_buf, sems.at[1]).wait()
    lane = lax.broadcasted_iota(jnp.int32, (16, CACHE), 1)
    row16 = lax.broadcasted_iota(jnp.int32, (16, CACHE), 0)
    ones_row = first_row((16, 128), 1.0).astype(BF16)

    def pack(source, count):
        length = length_ref[source]
        bias = jnp.where((row16 == 0) & (lane >= length), DEAD, 0.0).astype(BF16)
        part = key_buf[source]
        turned = jnp.concatenate([part, part, part, bias], 0).T
        for block in range(3):
            at = slice(block * 128, block * 128 + 128)
            keys[count + block] = turned[at]
            values[count + block] = jnp.concatenate([value_buf[source, :, at], ones_row], 0)
        return count + (length + 127) // 128

    count = lax.fori_loop(0, PLANE, pack, jnp.int32(0), unroll=2)
    dead_lane = lax.broadcasted_iota(jnp.int32, (128, 256), 1) == 3 * HD
    for block in range(KB // 128):
        keys[count + block] = jnp.where(dead_lane, DEAD, 0.0).astype(BF16)
        values[count + block] = jnp.zeros((96, 128), BF16)
    chunks = (count + KB // 128 - 1) // (KB // 128)

    for first in range(0, SLOTS, GS):
        here = jnp.where((first >= 8) & (group == 1), 0, chunks)
        for slot in range(first, first + GS):
            max_ref[slot] = max_in[slot]
            acc_ref[slot] = acc_in[slot]

        def chunk(step, carry, first=first):
            per = KB // 128
            key_part = jnp.concatenate([keys[per * step + block] for block in range(per)], 0)
            value_part = jnp.concatenate([values[per * step + block] for block in range(per)], 1)
            for slot in range(first, first + GS):
                max_ref[slot], acc_ref[slot] = flash_step(
                    query_ref[slot], key_part, value_part, max_ref[slot], acc_ref[slot]
                )
            return carry

        lax.fori_loop(0, here, chunk, 0)

        for slot in range(first, first + GS):
            acc = acc_ref[slot]
            total = jnp.where(here > 0, acc[HD : HD + 1], 1.0)
            pieces = split3(max_ref[slot] + jnp.log2(total))
            target, at = (sent_ref, slot) if slot < SENT else (kept_ref, slot - SENT)
            row = lax.broadcasted_iota(jnp.int32, (16, TILE), 0)
            tail = jnp.where(
                row == 0,
                pieces[0].astype(F32),
                jnp.where(row == 1, pieces[1].astype(F32), pieces[2].astype(F32)),
            )
            tail = jnp.where(row <= 2, tail, 0.0)
            target[at] = jnp.concatenate([acc[0:HD] / total, tail], 0).astype(BF16)


def cached(where, lengths, mine, peer, query, top, acc):
    return pl.pallas_call(
        cached_kernel,
        out_shape=[
            jax.ShapeDtypeStruct((SENT, 96, TILE), BF16),
            jax.ShapeDtypeStruct((SLOTS - SENT, 96, TILE), BF16),
        ],
        in_specs=[sm(), sm(), anyspace(), anyspace(), vm(), vm(), vm()],
        out_specs=[vm(), vm()],
        scratch_shapes=[
            pltpu.VMEM((PLANE, HD, CACHE), BF16),
            pltpu.VMEM((PLANE, HD, CACHE), BF16),
            pltpu.VMEM((BLOCKS, 128, 256), BF16),
            pltpu.VMEM((BLOCKS, 96, 128), BF16),
            pltpu.VMEM((SLOTS, 1, TILE), F32),
            pltpu.VMEM((SLOTS, 96, TILE), F32),
            pltpu.SemaphoreType.DMA((2,)),
        ],
        compiler_params=params(),
        name="cached",
    )(where, lengths, mine, peer, query, top, acc)


def spread_kernel(where_ref, sent_ref, kept_ref, got_ref, dec_ref, own_ref, out_ref):
    group = where_ref[0]
    plane = where_ref[1]

    @pl.when(group == 0)
    def _():
        for slot, tile in enumerate(TILES[0]):
            part = sent_ref[slot] if slot < SENT else kept_ref[slot - SENT]
            out_ref[2 * tile] = part[:, 0:ROWS]
            out_ref[2 * tile + 1] = part[:, ROWS:]
        for slot, tile in enumerate(TILES[1][:SENT]):
            part = got_ref[slot]
            out_ref[2 * tile] = part[:, 0:ROWS]
            out_ref[2 * tile + 1] = part[:, ROWS:]

    @pl.when(group == 1)
    def _():
        wide = jnp.concatenate([kept_ref[0], kept_ref[1]], 1)

        def pick(index):
            return jnp.dot(wide, decode_choice(dec_ref[index]), preferred_element_type=F32)

        def plain(item, carry):
            index = (1 - plane) * PLANE + item
            out_ref[index] = pick(index).astype(BF16)
            return carry

        lax.fori_loop(0, PLANE, plain, 0, unroll=2)

        def joined(item, carry):
            index = plane * PLANE + item
            picked = pick(index)
            here = picked[HD : HD + 1] + picked[HD + 1 : HD + 2] + picked[HD + 2 : HD + 3]
            own = own_ref[item]
            there = own[HD : HD + 1]
            top = jnp.maximum(here, there)
            left = jnp.exp2(here - top)
            right = jnp.exp2(there - top)
            total = left + right
            value = (picked[0:HD] * left + own[0:HD] * right) / total
            high, mid, low = split3(top + jnp.log2(total))
            row = lax.broadcasted_iota(jnp.int32, (16, ROWS), 0)
            tail = jnp.where(
                row == 0,
                high.astype(F32),
                jnp.where(row == 1, mid.astype(F32), low.astype(F32)),
            )
            tail = jnp.where(row <= 2, tail, 0.0)
            out_ref[index] = jnp.concatenate([value, tail], 0).astype(BF16)
            return carry

        lax.fori_loop(0, PLANE, joined, 0, unroll=2)


def spread(where, sent, kept, got, dec, own):
    return pl.pallas_call(
        spread_kernel,
        out_shape=jax.ShapeDtypeStruct((N_CTX, 96, ROWS), BF16),
        in_specs=[sm()] + [vm()] * 5,
        out_specs=vm(),
        compiler_params=params(),
        name="spread",
    )(where, sent, kept, got, dec, own)


def join_kernel(parts_ref, out_ref, wide):
    for head in range(PLANE):
        first = parts_ref[head].astype(F32)
        second = parts_ref[PLANE + head].astype(F32)
        one = first[HD : HD + 1] + first[HD + 1 : HD + 2] + first[HD + 2 : HD + 3]
        two = second[HD : HD + 1] + second[HD + 1 : HD + 2] + second[HD + 2 : HD + 3]
        top = jnp.maximum(one, two)
        left = jnp.exp2(one - top)
        right = jnp.exp2(two - top)
        total = left + right
        wide[head * HD : head * HD + HD, :] = (
            first[0:HD] * (left / total) + second[0:HD] * (right / total)
        )
    for block in range(HALF // 128):
        lanes = slice(block * 128, block * 128 + 128)
        out_ref[:, lanes] = wide[lanes, :].T.astype(BF16)


def join(parts):
    return pl.pallas_call(
        join_kernel,
        out_shape=jax.ShapeDtypeStruct((ROWS, HALF), BF16),
        in_specs=[vm()],
        out_specs=vm(),
        scratch_shapes=[pltpu.VMEM((HALF, ROWS), F32)],
        compiler_params=params(),
        name="join",
    )(parts)


def angle_tables(offset):
    quarter = HD // 4
    frequency = 10000.0 ** (-jnp.arange(quarter, dtype=F32) / quarter)
    lane = jnp.arange(TILE, dtype=jnp.int32)
    step = jnp.arange(STEPS, dtype=jnp.int32)
    base = offset // PROT
    column = jnp.concatenate([(offset + lane) % PROT, (offset + PLANE * TILE + step) % PROT])
    homolog = base + jnp.arange(20, dtype=jnp.int32)
    column_angle = frequency[:, None] * column.astype(F32)[None]
    homolog_angle = frequency[:, None] * homolog.astype(F32)[None]
    carry = (offset % PROT + lane) >= PROT
    step_homolog = (offset + PLANE * TILE + step) // PROT - base

    def tiles(function):
        columns = function(column_angle)
        homologs = function(homolog_angle)
        low = homologs[:, 0:16].T[:, :, None]
        high = homologs[:, 1:17].T[:, :, None]
        second = jnp.where(carry[None, None, :], high, low)
        first = jnp.broadcast_to(columns[None, :, :TILE], second.shape)
        whole = jnp.concatenate([first, first, second, second], 1)
        pick = (jnp.arange(20)[:, None] == step_homolog[None, :]).astype(F32)
        dec_second = jnp.sum(homologs[:, :, None] * pick[None], 1)
        dec_first = columns[:, TILE:]
        dec = jnp.concatenate([dec_first, dec_first, dec_second, dec_second], 0)
        dec = jnp.repeat(dec, VOCAB, axis=1).reshape(HD, 2, TILE).transpose(1, 0, 2)
        return jnp.concatenate([whole, dec], 0)

    return tiles(jnp.cos), tiles(jnp.sin)


def local(
    token_ids,
    span_offset,
    shard_lengths,
    embed_table,
    norm_gain,
    query_weight,
    key_weight,
    value_weight,
    cache_keys,
    cache_values,
):
    group = lax.axis_index("group")
    plane = lax.axis_index("yh")
    head = lax.axis_index("zx")
    mp = lax.axis_index("mp")
    tiles = jnp.where(group == 0, jnp.array(TILES[0], jnp.int32), jnp.array(TILES[1], jnp.int32))
    where = jnp.concatenate([jnp.stack([group, plane, mp, head]).astype(jnp.int32), tiles])
    swap = [(0, 1), (1, 0)]

    turned = turn(where, cache_keys, cache_values).reshape(PLANE, HD, CACHE)
    mine = lax.all_to_all(turned, "zx", 0, 0, tiled=True)
    peer = lax.ppermute(mine, "group", swap)

    small = jnp.concatenate([token_ids, jnp.broadcast_to(shard_lengths[None], (1, 128))], 0)
    small = jnp.broadcast_to(small[None], (N_CTX, 2, 128))
    small = lax.all_to_all(small, ("yh", "zx"), 0, 0, tiled=True)
    mine_ids = small[:, 0]
    lengths = lax.dynamic_slice(small[:, 1, 0], (plane * PLANE,), (PLANE,))
    prefill_ids = lax.ppermute(mine_ids, "group", [(0, 1)])
    prefill_ids = jnp.where(group == 0, mine_ids, prefill_ids)
    decode_ids = mine_ids.reshape(N_CTX, 1, ROWS)
    table_ids = jnp.broadcast_to(jnp.arange(TILE, dtype=jnp.int32) % VOCAB, (2, TILE))
    ids = jnp.concatenate([prefill_ids.reshape(PLANE, TILE), table_ids], 0)[:, None, :]

    wide_embed = embed_table.astype(F32)
    square = jnp.sum(wide_embed * wide_embed, 1)
    square = square + lax.ppermute(square, "mp", swap)
    own, other = table(
        where,
        embed_table,
        norm_gain[None],
        square[:, None],
        query_weight,
        key_weight,
        value_weight,
    )
    recv = lax.ppermute(other, "mp", swap)
    cosine, sine = angle_tables(span_offset[0])
    query, top, acc, own_part = fresh(where, own, recv, ids, decode_ids, cosine, sine)
    sent, kept = cached(where, lengths, mine, peer, query, top, acc)
    got = lax.ppermute(sent, "group", [(1, 0)])
    blocks = spread(where, sent, kept, got, decode_ids, own_part)
    parts = lax.all_to_all(blocks, ("yh", "zx"), 0, 0, tiled=True)
    return join(parts)[None]


def solution(mesh):
    inner = Mesh(mesh.devices.reshape(2, 2, PLANE, 2), ("group", "yh", "zx", "mp"))
    ctx = ("yh", "zx")
    placed = (
        P("group", ctx),
        P(),
        P(ctx),
        P(None, "mp"),
        P("mp"),
        P("mp", None),
        P("mp", None),
        P("mp", None),
        P(ctx, "mp"),
        P(ctx, "mp"),
    )
    return jax.shard_map(
        local, mesh=inner, in_specs=placed, out_specs=P("group", ctx, "mp"), check_vma=False
    )
```

time: 1000 us -> 148 us (0.15)
  the two profiles are of different devices: /device:TPU:106 before, /device:TPU:1 now
where the time goes in v1:
time: 148 us
  Pallas kernels  71.6 us (48%)
  starting transfers between devices  23.9 us (16%)
  waiting for transfers between devices  19.7 us (13%)
  blocking collectives  18.3 us (12%)
  local copies, waits for them, and re-layouts  7.43 us (5%)
  other arithmetic  5.23 us (4%)
  between operations  1.69 us (1%)
    pallas_call x1, Pallas kernels, cached(): pl.pallas_call(cached_kernel, out_shape=[jax.ShapeDtypeStruct((SENT, 96,...  29.4 us
    pallas_call x1, Pallas kernels, fresh(): pl.pallas_call(fresh_kernel, out_shape=[jax.ShapeDtypeStruct((SLOTS, 256,...  25.2 us
    all_to_all x1, blocking collectives, local(): parts = lax.all_to_all(blocks, ('yh', 'zx'), 0, 0, tiled=True)  18.3 us
    all_to_all x1, waiting for transfers between devices, local(): mine = lax.all_to_all(turned, 'zx', 0, 0, tiled=True)  12.5 us
    all_to_all x1, starting transfers between devices, local(): mine = lax.all_to_all(turned, 'zx', 0, 0, tiled=True)  7.61 us
    all_to_all x1, starting transfers between devices, local(): small = lax.all_to_all(small, ('yh', 'zx'), 0, 0, tiled=True)  6.8 us
    pallas_call x1, Pallas kernels, spread(): pl.pallas_call(spread_kernel, out_shape=jax.ShapeDtypeStruct((N_CTX, 96,...  5.95 us
    pallas_call x1, Pallas kernels, table(): pl.pallas_call(table_kernel, out_shape=[jax.ShapeDtypeStruct((3 * HD, VOC...  5.77 us
  transfers between devices with their start and end apart: 7, of which 4 were waited for; matrix products, arithmetic and copies ran while one was open for 6% of the time, Pallas kernels for 23%

profile of v1, /device:TPU:1, one launch (start us, length us, event | category | flops | bytes accessed | tf_op | source)
XLA Modules:
  0.0 147.8 jit_solution(7840887174317254109)
XLA Ops:
  0.0 1.1 multiply_reduce_fusion
  1.1 2.2 %collective-permute-start.1 = (f32[128]{0:T(128)S(1)}, f32[128]{0:T(128)S(1)}, u32[]{:S(2)}, u32[]{:S(2)}) collective-permute-start(f32[128]{0:T(128)S(1)} %multiply_reduce_fusion), channel_id=1, source_target_pairs={{0,1},{1,0},{2,3},{3,2},{4,5},{5,4},{6,7},{7,6},{8,9},{9,8},{10,11... | collective-permute-start | bytes 1544 | tf_op jit(solution)/shard_map/ppermute | solution.py:588
  3.3 0.7 broadcast_select_fusion.3
  4.0 0.6 concatenate.34.where_ref
  4.6 3.1 %turn.1 = bf16[1280,384]{1,0:T(8,128)(2,1)} custom-call(s32[14]{0:T(128)} %concatenate.34.where_ref, bf16[384,1280]{1,0:T(8,128)(2,1)} %keys_ref.1, bf16[384,1280]{1,0:T(8,128)(2,1)} %values_ref.1), custom_call_target="tpu_custom_call" | custom-call | tf_op jit(solution)/shard_map/turn/pallas_call | solution.py:78
  7.7 0.0 copy-start.6
  7.7 7.6 %all-to-all-start.1 = ((bf16[16,80,384]{2,1,0:T(8,128)(2,1)}), bf16[16,80,384]{2,1,0:T(8,128)(2,1)S(1)}, u32[]{:S(2)}, u32[]{:S(2)}) async-start(bf16[16,80,384]{2,1,0:T(8,128)(2,1)} %bitcast.32), calls=%async_computation.1 | async-start | bytes 1966080 | tf_op jit(solution)/shard_map/all_to_all | solution.py:572
  16.8 0.1 multiply_cosine_fusion.1
  16.9 0.1 copy.44
  17.0 0.1 copy.46
  17.1 0.2 multiply_sine_fusion
  17.4 0.0 copy-done.6
  17.4 0.1 fusion
  17.5 0.1 multiply_reduce_fusion.1
  17.6 0.3 broadcast_select_fusion
  17.9 12.5 %all-to-all-done.1.mine_ref = bf16[16,80,384]{2,1,0:T(8,128)(2,1)S(1)} async-done(((bf16[16,80,384]{2,1,0:T(8,128)(2,1)}), bf16[16,80,384]{2,1,0:T(8,128)(2,1)S(1)}, u32[]{:S(2)}, u32[]{:S(2)}) %all-to-all-start.1) | async-done | bytes 983072 | tf_op jit(solution)/shard_map/all_to_all | solution.py:572
  30.4 0.0 copy-start
  30.4 0.7 broadcast_in_dim.101
  31.1 6.8 %all-to-all-start = ((s32[32,2,128]{2,1,0:T(2,128)}), s32[32,2,128]{2,1,0:T(2,128)S(1)}, u32[]{:S(2)}, u32[]{:S(2)}) async-start(s32[32,2,128]{2,1,0:T(2,128)} %broadcast_in_dim.101), calls=%async_computation | async-start | bytes 65536 | tf_op jit(solution)/shard_map/all_to_all | solution.py:577
  37.9 1.2 collective-permute-start
  39.2 0.1 broadcast_in_dim.114
  39.3 0.1 reshape_reshape.7
  39.5 0.1 broadcast_in_dim.110
  39.6 0.1 reshape_reshape.6
  39.8 1.3 pad_maximum_fusion.1.sin_ref
  41.1 0.0 copy-done
  41.1 0.0 copy-start.5
  41.2 1.3 pad_maximum_fusion.cos_ref
  42.4 0.0 copy-done.5
  42.4 0.6 broadcast_in_dim.102.gain_ref
  43.0 3.5 %all-to-all-done = s32[32,2,128]{2,1,0:T(2,128)S(1)} async-done(((s32[32,2,128]{2,1,0:T(2,128)}), s32[32,2,128]{2,1,0:T(2,128)S(1)}, u32[]{:S(2)}, u32[]{:S(2)}) %all-to-all-start) | async-done | bytes 32800 | tf_op jit(solution)/shard_map/all_to_all | solution.py:577
  46.6 0.0 copy-start.3
  46.6 1.3 collective-permute-start.3
  47.9 0.0 collective-permute-done.1
  47.9 0.7 copy.43.square_ref
  48.6 5.8 %table.1 = (f32[240,128]{1,0:T(8,128)}, f32[240,128]{1,0:T(8,128)}) custom-call(s32[14]{0:T(128)} %concatenate.34.where_ref, bf16[128,1280]{1,0:T(8,128)(2,1)} %embed_ref.1, bf16[1,1280]{1,0:T(2,128)(2,1)} %broadcast_in_dim.102.gain_ref, f32[128,1]{1,0:T(8,128)} %copy.43.square_ref, bf16[1280,2560]{1,0:T(8,128)(2,1)} %wq.1, bf16[1280,2560]{1,0:T(8,128)(2,1)} %wk.1, ...), custom_call_target="tpu_custom_call" | custom-call | tf_op jit(solution)/shard_map/table/pallas_call | solution.py:116
  54.4 0.1 collective-permute-start.2
  54.5 1.0 dynamic-slice_reduce_fusion.length_ref
  55.5 0.0 collective-permute-done.3
  55.5 0.0 copy-done.3
  55.6 0.6 broadcast_in_dim.105.ids_ref
  56.2 2.3 %collective-permute-done.2.recv_ref = f32[240,128]{1,0:T(8,128)S(1)} collective-permute-done((f32[240,128]{1,0:T(8,128)}, f32[240,128]{1,0:T(8,128)S(1)}, u32[]{:S(2)}, u32[]{:S(2)}) %collective-permute-start.2) | collective-permute-done | bytes 122912 | tf_op jit(solution)/shard_map/ppermute | solution.py:598
  58.4 0.0 copy-start.4
  58.4 0.7 copy-done.4
  59.1 25.2 %fresh.1 = (bf16[10,256,256]{2,1,0:T(8,128)(2,1)}, f32[10,1,256]{2,1,0:T(1,128)}, f32[10,96,256]{2,1,0:T(8,128)}, f32[16,88,128]{2,1,0:T(8,128)}) custom-call(s32[14]{0:T(128)} %concatenate.34.where_ref, f32[240,128]{1,0:T(8,128)} %get-tuple-element.13.own_ref, f32[240,128]{1,0:T(8,128)} %copy-done.4, s32[18,1,256]{2,1,0:T(1,128)} %broadcast_in_dim.105.ids_ref, ...), custom_call_target="tpu_custom_call" | custom-call | tf_op jit(solution)/shard_map/fresh/pallas_call | solution.py:292
  84.3 0.0 collective-permute-done.peer_ref
  84.3 0.0 copy-start.1
  84.3 0.9 copy-done.1
  85.2 29.4 %cached.1 = (bf16[6,96,256]{2,1,0:T(8,128)(2,1)}, bf16[4,96,256]{2,1,0:T(8,128)(2,1)}) custom-call(s32[14]{0:T(128)} %concatenate.34.where_ref, s32[16]{0:T(128)} %dynamic-slice_reduce_fusion.length_ref, bf16[16,80,384]{2,1,0:T(8,128)(2,1)} %copy-done, bf16[16,80,384]{2,1,0:T(8,128)(2,1)} %copy-done.1, bf16[10,256,256]{2,1,0:T(8,128)(2,1)} %get-tuple-element.15.query_ref, ...), custom_call_target="tpu_custom_call" | custom-call | tf_op jit(solution)/shard_map/cached/pallas_call | solution.py:403
  114.7 4.6 %collective-permute-start.4 = (bf16[6,96,256]{2,1,0:T(8,128)(2,1)}, bf16[6,96,256]{2,1,0:T(8,128)(2,1)S(1)}, u32[]{:S(2)}, u32[]{:S(2)}) collective-permute-start(bf16[6,96,256]{2,1,0:T(8,128)(2,1)} %get-tuple-element.18.sent_ref), channel_id=1, source_target_pairs={{64,0},{65,1},{66,2},{67,3},{68,4},{69,5},{70,6},{71,7},{72,8},{73... | collective-permute-start | bytes 884744 | tf_op jit(solution)/shard_map/ppermute | solution.py:602
  119.3 1.4 collective-permute-done.4.got_ref
  120.7 0.0 copy-start.2
  120.7 0.7 copy-done.2
  121.4 6.0 %spread.1 = bf16[32,96,128]{2,1,0:T(8,128)(2,1)} custom-call(s32[14]{0:T(128)} %concatenate.34.where_ref, bf16[6,96,256]{2,1,0:T(8,128)(2,1)} %get-tuple-element.18.sent_ref, bf16[4,96,256]{2,1,0:T(8,128)(2,1)} %get-tuple-element.19.kept_ref, bf16[6,96,256]{2,1,0:T(8,128)(2,1)} %copy-done.2, s32[32,1,128]{2,1,0:T(1,128)} %copy-done.3, ...), custom_call_target="tpu_custom_call" | custom-call | tf_op jit(solution)/shard_map/spread/pallas_call | solution.py:480
  127.4 18.3 %all_to_all.15.parts_ref = bf16[32,96,128]{2,1,0:T(8,128)(2,1)} all-to-all(bf16[32,96,128]{2,1,0:T(8,128)(2,1)} %spread.1), channel_id=1, replica_groups=mesh['group'=2,'yh'=2,'zx'=16,'mp'=2] {'yh','zx'}, dimensions={0} | all-to-all | bytes 1572864 | tf_op jit(solution)/shard_map/all_to_all | solution.py:604
  145.6 2.1 %join.1 = bf16[128,1280]{1,0:T(8,128)(2,1)} custom-call(bf16[32,96,128]{2,1,0:T(8,128)(2,1)} %all_to_all.15.parts_ref), custom_call_target="tpu_custom_call" | custom-call | tf_op jit(solution)/shard_map/join/pallas_call | solution.py:509
  (26 shorter events, 0.2 us)
Async XLA Ops:
  1.1 46.8 %collective-permute-start.1 = (f32[128]{0:T(128)S(1)}, f32[128]{0:T(128)S(1)}, u32[]{:S(2)}, u32[]{:S(2)}) collective-permute-start(f32[128]{0:T(128)S(1)} %multiply_reduce_fusion), channel_id=1, source_target_pairs={{0,1},{1,0},{2,3},{3,2},{4,5},{5,4},{6,7},{7,6},{8,9},{9,8},{10,11... | collective-permute-start | bytes 1544 | tf_op jit(solution)/shard_map/ppermute | solution.py:588
  7.7 9.6 %copy-start.6 = (s32[1,128]{1,0:T(1,128)S(1)}, s32[1,128]{1,0:T(1,128)}, u32[]{:S(2)}) copy-start(s32[1,128]{1,0:T(1,128)} %param.12) | copy-start | bytes 1540
  7.7 22.7 %all-to-all-start.1 = ((bf16[16,80,384]{2,1,0:T(8,128)(2,1)}), bf16[16,80,384]{2,1,0:T(8,128)(2,1)S(1)}, u32[]{:S(2)}, u32[]{:S(2)}) async-start(bf16[16,80,384]{2,1,0:T(8,128)(2,1)} %bitcast.32), calls=%async_computation.1 | async-start | bytes 1966080 | tf_op jit(solution)/shard_map/all_to_all | solution.py:572
  30.4 10.7 %copy-start = (bf16[16,80,384]{2,1,0:T(8,128)(2,1)}, bf16[16,80,384]{2,1,0:T(8,128)(2,1)S(1)}, u32[]{:S(2)}) copy-start(bf16[16,80,384]{2,1,0:T(8,128)(2,1)S(1)} %all-to-all-done.1.mine_ref) | copy-start | bytes 2949124
  31.1 15.5 %all-to-all-start = ((s32[32,2,128]{2,1,0:T(2,128)}), s32[32,2,128]{2,1,0:T(2,128)S(1)}, u32[]{:S(2)}, u32[]{:S(2)}) async-start(s32[32,2,128]{2,1,0:T(2,128)} %broadcast_in_dim.101), calls=%async_computation | async-start | bytes 65536 | tf_op jit(solution)/shard_map/all_to_all | solution.py:577
  37.9 46.4 %collective-permute-start = (bf16[16,80,384]{2,1,0:T(8,128)(2,1)S(1)}, bf16[16,80,384]{2,1,0:T(8,128)(2,1)S(1)}, u32[]{:S(2)}, u32[]{:S(2)}) collective-permute-start(bf16[16,80,384]{2,1,0:T(8,128)(2,1)S(1)} %all-to-all-done.1.mine_ref), channel_id=1, source_target_pairs={{0,64},{64,0},{1,65},{65,1},{2,66},{66,2},{3,67},{67,3},{4,68},{68... | collective-permute-start | bytes 2949128 | tf_op jit(solution)/shard_map/ppermute | solution.py:573
  41.1 1.3 copy-start.5
  46.6 8.9 %copy-start.3 = (s32[32,1,128]{2,1,0:T(1,128)}, s32[32,1,128]{2,1,0:T(1,128)S(1)}, u32[]{:S(2)}) copy-start(s32[32,1,128]{2,1,0:T(1,128)S(1)} %slice.41.dec_ref) | copy-start | bytes 49156
  46.6 8.9 %collective-permute-start.3 = (s32[32,128]{1,0:T(8,128)S(1)}, s32[32,128]{1,0:T(8,128)S(1)}, u32[]{:S(2)}, u32[]{:S(2)}) collective-permute-start(s32[32,128]{1,0:T(8,128)S(1)} %bitcast.35), channel_id=1, source_target_pairs={{0,64},{1,65},{2,66},{3,67},{4,68},{5,69},{6,70},{7,71},{8,72},{9,... | collective-permute-start | bytes 49160 | tf_op jit(solution)/shard_map/ppermute | solution.py:580
  54.4 4.0 %collective-permute-start.2 = (f32[240,128]{1,0:T(8,128)}, f32[240,128]{1,0:T(8,128)S(1)}, u32[]{:S(2)}, u32[]{:S(2)}) collective-permute-start(f32[240,128]{1,0:T(8,128)} %get-tuple-element.14), channel_id=1, source_target_pairs={{0,1},{1,0},{2,3},{3,2},{4,5},{5,4},{6,7},{7,6},{8,9},{9,8},{10,11... | collective-permute-start | bytes 368648 | tf_op jit(solution)/shard_map/ppermute | solution.py:598
  58.4 0.7 copy-start.4
  84.3 0.9 copy-start.1
  114.7 6.0 %collective-permute-start.4 = (bf16[6,96,256]{2,1,0:T(8,128)(2,1)}, bf16[6,96,256]{2,1,0:T(8,128)(2,1)S(1)}, u32[]{:S(2)}, u32[]{:S(2)}) collective-permute-start(bf16[6,96,256]{2,1,0:T(8,128)(2,1)} %get-tuple-element.18.sent_ref), channel_id=1, source_target_pairs={{64,0},{65,1},{66,2},{67,3},{68,4},{69,5},{70,6},{71,7},{72,8},{73... | collective-permute-start | bytes 884744 | tf_op jit(solution)/shard_map/ppermute | solution.py:602
  120.7 0.7 copy-start.2

commit v2 on v1

v2 whole, which is shorter than its diff:
```python
import math

import jax
import jax.numpy as jnp
from jax import lax
from jax.experimental import pallas as pl
from jax.experimental.pallas import tpu as pltpu
from jax.sharding import Mesh
from jax.sharding import PartitionSpec as P

D = 2560
HALF = 1280
HD = 80
PROT = 256
STEPS = 4
VOCAB = 128
PLANE = 16
N_CTX = 32
ROWS = 128
CACHE = 384
CHUNK = 88
TILE = 256
SLOTS = 10
SENT = 6
KB = 1024
GROUPS = ((0, 4), (4, 8), (8, 10))
FAR = 96.0
SCALE2 = math.log2(math.e) / math.sqrt(HD)
LOW = -1e30
DEAD = -2e30
F32 = jnp.float32
BF16 = jnp.bfloat16
TILES = ((0, 1, 2, 3, 10, 11, 12, 13, 14, 15), (4, 5, 6, 7, 8, 9, 16, 17, 0, 0))


def vm():
    return pl.BlockSpec(memory_space=pltpu.MemorySpace.VMEM)


def sm():
    return pl.BlockSpec(memory_space=pltpu.MemorySpace.SMEM)


def anyspace():
    return pl.BlockSpec(memory_space=pl.ANY)


def far():
    return pl.BlockSpec(memory_space=pltpu.MemorySpace.HBM)


def params(mib):
    return pltpu.CompilerParams(vmem_limit_bytes=mib << 20)


def split3(x):
    high = x.astype(BF16)
    rest = x - high.astype(F32)
    mid = rest.astype(BF16)
    low = (rest - mid.astype(F32)).astype(BF16)
    return high, mid, low


def first_row(shape, value):
    return jnp.where(lax.broadcasted_iota(jnp.int32, shape, 0) == 0, value, 0.0)


def turn_kernel(where_ref, small_ref, keys_ref, values_ref, out_ref, buf, sem):
    @pl.when(where_ref[0] == 0)
    def _():
        pltpu.make_async_copy(keys_ref, buf, sem).start()

    @pl.when(where_ref[0] != 0)
    def _():
        pltpu.make_async_copy(values_ref, buf, sem).start()

    small = small_ref[...].astype(BF16)
    for head in range(PLANE):
        out_ref[head, HD:] = small
    pltpu.make_async_copy(keys_ref, buf, sem).wait()
    for block in range(HALF // 128):
        part = buf[:, block * 128 : block * 128 + 128].T
        row = block * 128
        while row < block * 128 + 128:
            head = row // HD
            end = min((head + 1) * HD, block * 128 + 128)
            out_ref[head, row - head * HD : end - head * HD] = part[
                row - block * 128 : end - block * 128
            ]
            row = end


def turn(where, small, keys, values):
    return pl.pallas_call(
        turn_kernel,
        out_shape=jax.ShapeDtypeStruct((PLANE, CHUNK, CACHE), BF16),
        in_specs=[sm(), vm(), far(), far()],
        out_specs=vm(),
        scratch_shapes=[pltpu.VMEM((CACHE, HALF), BF16), pltpu.SemaphoreType.DMA(())],
        compiler_params=params(56),
        name="turn",
    )(where, small, keys, values)


def gate_kernel(value_ref, earlier_ref, out_ref):
    del value_ref, earlier_ref, out_ref


def gate(value, earlier):
    return pl.pallas_call(
        gate_kernel,
        out_shape=jax.ShapeDtypeStruct(value.shape, value.dtype),
        in_specs=[anyspace(), anyspace()],
        out_specs=anyspace(),
        input_output_aliases={0: 0},
        name="gate",
    )(value, earlier)


def table_kernel(where_ref, embed_ref, gain_ref, square_ref, wq, wk, wv, own_ref, other_ref, buf, turned, sems):
    mp = where_ref[2]
    head = where_ref[3]
    base = jnp.minimum((head * HD) // 128 * 128, 1024)
    inside = pl.multiple_of(head * HD - base, 16)
    halves = (mp, 1 - mp)
    for half in range(2):
        at = pl.multiple_of(halves[half] * HALF + base, 128)
        for which, weight in enumerate((wq, wk, wv)):
            pltpu.make_async_copy(
                weight.at[:, pl.ds(at, 256)], buf.at[half * 3 + which], sems.at[half * 3 + which]
            ).start()
    mean = square_ref[...] / D
    normal = (
        embed_ref[...].astype(F32) * lax.rsqrt(mean + 1e-05) * gain_ref[...].astype(F32)
    ).astype(BF16)
    for half in (1, 0):
        for which in range(3):
            pltpu.make_async_copy(
                wq.at[:, pl.ds(0, 256)], buf.at[half * 3 + which], sems.at[half * 3 + which]
            ).wait()
            turned[...] = jnp.dot(normal, buf[half * 3 + which], preferred_element_type=F32).T
            out = own_ref if half == 0 else other_ref
            out[which * HD : which * HD + HD, :] = turned[pl.ds(inside, HD), :]


def table(where, embed, gain, square, wq, wk, wv):
    return pl.pallas_call(
        table_kernel,
        out_shape=[jax.ShapeDtypeStruct((3 * HD, VOCAB), F32)] * 2,
        in_specs=[sm(), vm(), vm(), vm(), far(), far(), far()],
        out_specs=[vm(), vm()],
        scratch_shapes=[
            pltpu.VMEM((6, HALF, 256), BF16),
            pltpu.VMEM((256, VOCAB), F32),
            pltpu.SemaphoreType.DMA((6,)),
        ],
        compiler_params=params(56),
        name="table",
    )(where, embed, gain, square, wq, wk, wv)


def fresh_kernel(
    where_ref,
    own_ref,
    recv_ref,
    mine_ref,
    column_ref,
    homolog_ref,
    step_ref,
    query_ref,
    max_ref,
    acc_ref,
    own_out,
    dec_ref,
    length_out,
    keys,
    values,
    wide,
    worst_ref,
    ids_ref,
):
    group = where_ref[0]
    plane = where_ref[1]
    quarter = HD // 4
    smalls = [mine_ref[source, HD:CHUNK, :].astype(F32) for source in range(PLANE)]
    sixteen = lax.broadcasted_iota(jnp.int32, (PLANE, 128), 0)
    length = jnp.zeros((PLANE, 128), F32)
    for source in range(PLANE):
        small = smalls[source]
        size = small[2:3, 0:128] * 16.0 + small[2:3, 128:256]
        length = jnp.where(sixteen == source, jnp.broadcast_to(size, (PLANE, 128)), length)
        for half in range(2):
            same = plane == half
            block = half * PLANE + source
            first = jnp.where(same, small[0:1, 0:128], small[0:1, 128:256])
            lanes = slice(source % 2 * ROWS, source % 2 * ROWS + ROWS)
            ids_ref[block // 2, :, lanes] = first.astype(jnp.int32)
            second = jnp.where(same, small[1:2, 0:128], small[1:2, 128:256])
            dec_ref[block] = second.astype(jnp.int32)
    length_out[...] = length.astype(jnp.int32)
    for part in range(2):
        ids_ref[PLANE + part] = lax.broadcasted_iota(jnp.int32, (1, TILE), 1) % VOCAB
    tables = own_ref[...] + recv_ref[...]
    row = lax.broadcasted_iota(jnp.int32, (HD, VOCAB), 0)
    upper = (row // quarter) % 2 == 0

    def stacked(part):
        partner = jnp.where(
            upper, -pltpu.roll(part, HD - quarter, 0), pltpu.roll(part, quarter, 0)
        )
        pieces = []
        for item in (part, partner):
            high = item.astype(BF16)
            pieces += [high, (item - high.astype(F32)).astype(BF16)]
        return jnp.concatenate(pieces, 0)

    query_table = stacked(tables[0:HD])
    key_table = stacked(tables[HD : 2 * HD])
    value_table = tables[2 * HD :].astype(BF16)
    tail_keys = jnp.zeros((16, TILE), BF16)
    ones_row = first_row((16, TILE), 1.0).astype(BF16)
    lane = lax.broadcasted_iota(jnp.int32, (1, TILE), 1)
    carried = lane + where_ref[14] >= PROT

    def chosen(tile):
        return (
            lax.broadcasted_iota(jnp.int32, (VOCAB, TILE), 0) == ids_ref[tile]
        ).astype(BF16)

    def homolog_at(which, tile):
        low = homolog_ref[which, tile]
        high = homolog_ref[which, tile + 1]
        return jnp.where(
            carried, jnp.concatenate([high, high], 1), jnp.concatenate([low, low], 1)
        )

    def turned_by(one_hot, stack, tile, decode=None):
        raw = jnp.dot(stack, one_hot, preferred_element_type=F32)
        plain = raw[0:HD] + raw[HD : 2 * HD]
        partner = raw[2 * HD : 3 * HD] + raw[3 * HD :]
        if decode is not None:
            return (plain * step_ref[0, decode] + partner * step_ref[1, decode]).astype(BF16)
        half = HD // 2
        first = plain[:half] * column_ref[0] + partner[:half] * column_ref[1]
        second = plain[half:] * homolog_at(0, tile) + partner[half:] * homolog_at(1, tile)
        return jnp.concatenate([first, second], 0).astype(BF16)

    def tile_of(slot):
        return where_ref[4 + slot]

    def put_query(slot, rotated):
        query_ref[slot] = jnp.concatenate([*split3(rotated.astype(F32) * SCALE2), ones_row], 0)

    def one_query(slot, carry):
        tile = tile_of(slot)
        put_query(slot, turned_by(chosen(tile), query_table, tile))
        return carry

    lax.fori_loop(0, jnp.where(group == 0, SLOTS, SENT), one_query, 0)

    def one_key(block, carry):
        tile = 2 * block + plane
        one_hot = chosen(tile)
        rotated = turned_by(one_hot, key_table, tile)
        keys[block] = jnp.concatenate([rotated, rotated, rotated, tail_keys], 0).T
        picked = jnp.dot(value_table, one_hot, preferred_element_type=F32).astype(BF16)
        values[block] = jnp.concatenate([picked, ones_row], 0)
        return carry

    lax.fori_loop(0, 8, one_key, 0, unroll=2)

    @pl.when(group == 1)
    def _():
        for part in range(2):
            lanes = slice(part * TILE, part * TILE + TILE)
            one_hot = chosen(16 + part)
            put_query(SENT + part, turned_by(one_hot, query_table, 0, part))
            query_ref[SENT + 2 + part] = jnp.zeros((256, TILE), BF16)
            wide[0 : 3 * HD, lanes] = query_ref[SENT + part, 0 : 3 * HD, :]
            wide[3 * HD : 4 * HD, lanes] = turned_by(one_hot, key_table, 0, part)
            wide[4 * HD : 5 * HD, lanes] = jnp.dot(
                value_table, one_hot, preferred_element_type=F32
            ).astype(BF16)


    def last_half(slot, half, state):
        tile = tile_of(slot)
        limit = jnp.where(tile >= PLANE, 1 << 20, tile * TILE) + lane
        top, acc = state
        scores = []
        for unit in range(4):
            block = 4 * half + unit
            part = jnp.dot(keys[block], query_ref[slot], preferred_element_type=F32)
            row_at = lax.broadcasted_iota(jnp.int32, (TILE, TILE), 0)
            seen = row_at + (2 * block + plane) * TILE <= limit
            scores.append(jnp.where(seen, part, DEAD))
        new = top
        for part in scores:
            new = jnp.maximum(new, jnp.max(part, 0, keepdims=True))
        total = None
        for unit in range(4):
            weights = jnp.exp2(scores[unit] - new).astype(BF16)
            piece = jnp.dot(values[4 * half + unit], weights, preferred_element_type=F32)
            total = piece if total is None else total + piece
        if acc is None:
            return new, total
        return new, acc * jnp.exp2(top - new) + total

    low_start = jnp.full((1, TILE), LOW, F32)

    def early(pair, carry):
        for slot in (2 * pair, 2 * pair + 1):
            max_ref[slot], acc_ref[slot] = last_half(slot, 0, (low_start, None))
        return carry

    lax.fori_loop(0, 2, early, 0)
    worst_ref[...] = jnp.zeros((1, TILE), F32)

    def late(pair, carry):
        for slot in (2 * pair, 2 * pair + 1):
            top, acc = last_half(slot, 1, (low_start, None))
            first = jnp.dot(keys[0], query_ref[slot], preferred_element_type=F32)
            base = jnp.maximum(top, jnp.max(first, 0, keepdims=True))
            new, total, peak = stale_units(
                [(keys[unit], values[unit]) for unit in range(4)], query_ref[slot], base
            )
            worst_ref[...] = jnp.maximum(worst_ref[...], peak - base)
            acc = acc * jnp.exp2(top - base) + total
            max_ref[slot] = new
            acc_ref[slot] = acc * jnp.exp2(base - new)
        return carry

    pairs = jnp.where(group == 0, SLOTS // 2, SLOTS // 2 - 1)
    lax.fori_loop(2, pairs, late, 0)

    @pl.when(jnp.max(worst_ref[...]) > FAR)
    def _():
        def again(slot, carry):
            state = last_half(slot, 1, (low_start, None))
            max_ref[slot], acc_ref[slot] = last_half(slot, 0, state)
            return carry

        lax.fori_loop(4, 2 * pairs, again, 0)

    @pl.when(group == 1)
    def _():
        key_at = lax.broadcasted_iota(jnp.int32, (TILE, TILE), 0)
        query_at = lax.broadcasted_iota(jnp.int32, (TILE, TILE), 1)
        seen = (key_at // STEPS == query_at // STEPS) & (key_at <= query_at)

        def one_block(item, carry):
            at = plane * PLANE + 2 * item
            one_hot = decode_choice(jnp.concatenate([dec_ref[at], dec_ref[at + 1]], 1))
            picked = jnp.dot(wide[...], one_hot, preferred_element_type=F32).astype(BF16)
            queries = jnp.concatenate([picked[0 : 3 * HD], ones_row], 0)
            own_keys = picked[3 * HD : 4 * HD]
            own_keys = jnp.concatenate([own_keys, own_keys, own_keys, tail_keys], 0).T
            scores = jnp.dot(own_keys, queries, preferred_element_type=F32)
            scores = jnp.where(seen, scores, DEAD)
            top = jnp.max(scores, 0, keepdims=True)
            weights = jnp.exp2(scores - top).astype(BF16)
            acc = jnp.dot(
                jnp.concatenate([picked[4 * HD :], ones_row], 0),
                weights,
                preferred_element_type=F32,
            )
            total = acc[HD : HD + 1]
            value = acc[0:HD] / total
            log_sum = jnp.broadcast_to(top + jnp.log2(total), (8, TILE))
            for part in range(2):
                lanes = slice(part * ROWS, part * ROWS + ROWS)
                own_out[2 * item + part, 0:HD] = value[:, lanes]
                own_out[2 * item + part, HD:88] = log_sum[:, lanes]
            return carry

        lax.fori_loop(0, PLANE // 2, one_block, 0, unroll=2)


def stale_units(units, query, base):
    peak = base
    total = None
    for key_part, value_part in units:
        scores = jnp.dot(key_part, query, preferred_element_type=F32)
        weights = jnp.exp2(scores - base).astype(BF16)
        peak = jnp.maximum(peak, jnp.max(scores, 0, keepdims=True))
        piece = jnp.dot(value_part, weights, preferred_element_type=F32)
        total = piece if total is None else total + piece
    return peak, total, peak


def decode_choice(ids):
    lane = lax.broadcasted_iota(jnp.int32, ids.shape, 1)
    wanted = (lane % STEPS) * VOCAB + ids
    rows = lax.broadcasted_iota(jnp.int32, (STEPS * VOCAB, ids.shape[1]), 0)
    return (rows == wanted).astype(BF16)


def fresh(where, own, recv, mine, column, homolog, step):
    return pl.pallas_call(
        fresh_kernel,
        out_shape=[
            jax.ShapeDtypeStruct((SLOTS, 256, TILE), BF16),
            jax.ShapeDtypeStruct((SLOTS, 1, TILE), F32),
            jax.ShapeDtypeStruct((SLOTS, 96, TILE), F32),
            jax.ShapeDtypeStruct((PLANE, 88, ROWS), F32),
            jax.ShapeDtypeStruct((N_CTX, 1, ROWS), jnp.int32),
            jax.ShapeDtypeStruct((PLANE, 128), jnp.int32),
        ],
        in_specs=[sm()] + [vm()] * 6,
        out_specs=[vm()] * 6,
        scratch_shapes=[
            pltpu.VMEM((8, TILE, 256), BF16),
            pltpu.VMEM((8, 96, TILE), BF16),
            pltpu.VMEM((5 * HD, STEPS * VOCAB), BF16),
            pltpu.VMEM((1, TILE), F32),
            pltpu.VMEM((PLANE + 2, 1, TILE), jnp.int32),
        ],
        compiler_params=params(20),
        name="fresh",
    )(where, own, recv, mine, column, homolog, step)


BLOCKS = PLANE * 3 + KB // 128 + 2


def cached_kernel(
    where_ref,
    length_ref,
    mine_ref,
    peer_ref,
    query_ref,
    max_in,
    acc_in,
    sent_ref,
    kept_ref,
    key_buf,
    value_buf,
    keys,
    values,
    max_ref,
    acc_ref,
    worst_ref,
    sems,
):
    group = where_ref[0]

    @pl.when(group == 0)
    def _():
        pltpu.make_async_copy(mine_ref, key_buf, sems.at[0]).start()
        pltpu.make_async_copy(peer_ref, value_buf, sems.at[1]).start()

    @pl.when(group != 0)
    def _():
        pltpu.make_async_copy(peer_ref, key_buf, sems.at[0]).start()
        pltpu.make_async_copy(mine_ref, value_buf, sems.at[1]).start()

    pltpu.make_async_copy(mine_ref, key_buf, sems.at[0]).wait()
    pltpu.make_async_copy(mine_ref, value_buf, sems.at[1]).wait()
    lane = lax.broadcasted_iota(jnp.int32, (16, CACHE), 1)
    row16 = lax.broadcasted_iota(jnp.int32, (16, CACHE), 0)
    ones_row = first_row((16, 128), 1.0).astype(BF16)

    def pack(source, count):
        length = length_ref[source, 0]
        bias = jnp.where((row16 == 0) & (lane >= length), DEAD, 0.0).astype(BF16)
        part = key_buf[source, 0:HD]
        turned = jnp.concatenate([part, part, part, bias], 0).T
        for block in range(3):
            at = slice(block * 128, block * 128 + 128)
            keys[count + block] = turned[at]
            values[count + block] = jnp.concatenate([value_buf[source, 0:HD, at], ones_row], 0)
        return count + (length + 127) // 128

    count = lax.fori_loop(0, PLANE, pack, jnp.int32(0), unroll=2)
    dead_lane = lax.broadcasted_iota(jnp.int32, (128, 256), 1) == 3 * HD
    for block in range(KB // 128):
        keys[count + block] = jnp.where(dead_lane, DEAD, 0.0).astype(BF16)
        values[count + block] = jnp.zeros((96, 128), BF16)
    chunks = (count + KB // 128 - 1) // (KB // 128)

    per = KB // 128
    starter = jnp.concatenate([keys[0], keys[1]], 0)
    worst_ref[...] = jnp.zeros((1, TILE), F32)

    def chunk_units(step):
        units = []
        for unit in range(per // 2):
            at = per * step + 2 * unit
            units.append(
                (
                    jnp.concatenate([keys[at], keys[at + 1]], 0),
                    jnp.concatenate([values[at], values[at + 1]], 1),
                )
            )
        return units

    for first, end in GROUPS:
        here = jnp.where((first >= 8) & (group == 1), 0, chunks)
        for slot in range(first, end):
            peak = jnp.max(
                jnp.dot(starter, query_ref[slot], preferred_element_type=F32), 0, keepdims=True
            )
            top = jnp.maximum(max_in[slot], peak)
            max_ref[slot] = top
            acc_ref[slot] = acc_in[slot] * jnp.exp2(max_in[slot] - top)

        def chunk(step, carry, first=first, end=end):
            units = chunk_units(step)
            for slot in range(first, end):
                base = max_ref[slot]
                new, total, peak = stale_units(units, query_ref[slot], base)
                worst_ref[...] = jnp.maximum(worst_ref[...], peak - base)
                max_ref[slot] = new
                acc_ref[slot] = (acc_ref[slot] + total) * jnp.exp2(base - new)
            return carry

        lax.fori_loop(0, here, chunk, 0)

    slots = jnp.where(group == 0, SLOTS, SLOTS - 2)

    @pl.when(jnp.max(worst_ref[...]) > FAR)
    def _():
        def one_slot(slot, carry):
            max_ref[slot] = max_in[slot]
            acc_ref[slot] = acc_in[slot]

            def one_chunk(block, inner):
                top = max_ref[slot]
                scores = jnp.dot(keys[block], query_ref[slot], preferred_element_type=F32)
                new = jnp.maximum(top, jnp.max(scores, 0, keepdims=True))
                weights = jnp.exp2(scores - new).astype(BF16)
                max_ref[slot] = new
                acc_ref[slot] = acc_ref[slot] * jnp.exp2(top - new) + jnp.dot(
                    values[block], weights, preferred_element_type=F32
                )
                return inner

            lax.fori_loop(0, count, one_chunk, 0)
            return carry

        lax.fori_loop(0, slots, one_slot, 0)

    row = lax.broadcasted_iota(jnp.int32, (16, TILE), 0)
    for slot in range(SLOTS):
        acc = acc_ref[slot]
        total = jnp.where(slot < slots, acc[HD : HD + 1], 1.0)
        high, mid, low = split3(max_ref[slot] + jnp.log2(total))
        target, at = (sent_ref, slot) if slot < SENT else (kept_ref, slot - SENT)
        tail = jnp.where(
            row == 0,
            high.astype(F32),
            jnp.where(row == 1, mid.astype(F32), low.astype(F32)),
        )
        tail = jnp.where(row <= 2, tail, 0.0)
        target[at] = jnp.concatenate([acc[0:HD] * (1.0 / total), tail], 0).astype(BF16)


def cached(where, lengths, mine, peer, query, top, acc):
    return pl.pallas_call(
        cached_kernel,
        out_shape=[
            jax.ShapeDtypeStruct((SENT, 96, TILE), BF16),
            jax.ShapeDtypeStruct((SLOTS - SENT, 96, TILE), BF16),
        ],
        in_specs=[sm(), sm(), anyspace(), anyspace(), vm(), vm(), vm()],
        out_specs=[vm(), vm()],
        scratch_shapes=[
            pltpu.VMEM((PLANE, CHUNK, CACHE), BF16),
            pltpu.VMEM((PLANE, CHUNK, CACHE), BF16),
            pltpu.VMEM((BLOCKS, 128, 256), BF16),
            pltpu.VMEM((BLOCKS, 96, 128), BF16),
            pltpu.VMEM((SLOTS, 1, TILE), F32),
            pltpu.VMEM((SLOTS, 96, TILE), F32),
            pltpu.VMEM((1, TILE), F32),
            pltpu.SemaphoreType.DMA((2,)),
        ],
        compiler_params=params(24),
        name="cached",
    )(where, lengths, mine, peer, query, top, acc)


def spread_kernel(where_ref, sent_ref, kept_ref, got_ref, dec_ref, own_ref, out_ref):
    group = where_ref[0]
    plane = where_ref[1]

    @pl.when(group == 0)
    def _():
        for slot, tile in enumerate(TILES[0]):
            part = sent_ref[slot] if slot < SENT else kept_ref[slot - SENT]
            out_ref[2 * tile] = part[:, 0:ROWS]
            out_ref[2 * tile + 1] = part[:, ROWS:]
        for slot, tile in enumerate(TILES[1][:SENT]):
            part = got_ref[slot]
            out_ref[2 * tile] = part[:, 0:ROWS]
            out_ref[2 * tile + 1] = part[:, ROWS:]

    @pl.when(group == 1)
    def _():
        wide = jnp.concatenate([kept_ref[0], kept_ref[1]], 1)

        def pick(index):
            ids = jnp.concatenate([dec_ref[index], dec_ref[index + 1]], 1)
            return jnp.dot(wide, decode_choice(ids), preferred_element_type=F32)

        def put(index, value):
            value = value.astype(BF16)
            out_ref[index] = value[:, 0:ROWS]
            out_ref[index + 1] = value[:, ROWS:]

        row = lax.broadcasted_iota(jnp.int32, (16, TILE), 0)

        def pair(item, carry):
            index = (1 - plane) * PLANE + 2 * item
            put(index, pick(index))
            index = plane * PLANE + 2 * item
            picked = pick(index)
            here = picked[HD : HD + 1] + picked[HD + 1 : HD + 2] + picked[HD + 2 : HD + 3]
            own = jnp.concatenate([own_ref[2 * item], own_ref[2 * item + 1]], 1)
            there = own[HD : HD + 1]
            top = jnp.maximum(here, there)
            left = jnp.exp2(here - top)
            right = jnp.exp2(there - top)
            total = left + right
            value = picked[0:HD] * (left / total) + own[0:HD] * (right / total)
            high, mid, low = split3(top + jnp.log2(total))
            tail = jnp.where(
                row == 0,
                high.astype(F32),
                jnp.where(row == 1, mid.astype(F32), low.astype(F32)),
            )
            tail = jnp.where(row <= 2, tail, 0.0)
            put(index, jnp.concatenate([value, tail], 0))
            return carry

        lax.fori_loop(0, PLANE // 2, pair, 0, unroll=2)


def spread(where, sent, kept, got, dec, own):
    return pl.pallas_call(
        spread_kernel,
        out_shape=jax.ShapeDtypeStruct((N_CTX, 96, ROWS), BF16),
        in_specs=[sm()] + [vm()] * 5,
        out_specs=vm(),
        compiler_params=params(12),
        name="spread",
    )(where, sent, kept, got, dec, own)


def join_kernel(parts_ref, out_ref, wide):
    for head in range(PLANE):
        first = parts_ref[head].astype(F32)
        second = parts_ref[PLANE + head].astype(F32)
        one = first[HD : HD + 1] + first[HD + 1 : HD + 2] + first[HD + 2 : HD + 3]
        two = second[HD : HD + 1] + second[HD + 1 : HD + 2] + second[HD + 2 : HD + 3]
        top = jnp.maximum(one, two)
        left = jnp.exp2(one - top)
        right = jnp.exp2(two - top)
        total = left + right
        wide[head * HD : head * HD + HD, :] = (
            first[0:HD] * (left / total) + second[0:HD] * (right / total)
        )
    for block in range(HALF // 128):
        lanes = slice(block * 128, block * 128 + 128)
        out_ref[:, lanes] = wide[lanes, :].T.astype(BF16)


def join(parts):
    return pl.pallas_call(
        join_kernel,
        out_shape=jax.ShapeDtypeStruct((ROWS, HALF), BF16),
        in_specs=[vm()],
        out_specs=vm(),
        scratch_shapes=[pltpu.VMEM((HALF, ROWS), F32)],
        compiler_params=params(8),
        name="join",
    )(parts)


def angle_tables(offset):
    quarter = HD // 4
    frequency = 10000.0 ** (-jnp.arange(quarter, dtype=F32) / quarter)
    lane = jnp.arange(TILE, dtype=jnp.int32)
    step = offset + PLANE * TILE + jnp.arange(STEPS, dtype=jnp.int32)
    homolog = offset // PROT + jnp.arange(PLANE + 1, dtype=jnp.int32)
    parts = [(offset + lane) % PROT, homolog, step % PROT, step // PROT]
    values = jnp.concatenate(parts).astype(F32)
    angle = jnp.tile(frequency, 2)[:, None] * values[None]
    both = jnp.stack([jnp.cos(angle), jnp.sin(angle)])
    column = both[:, :, :TILE]
    end = TILE + PLANE + 1
    homologs = both[:, :, TILE:end].transpose(0, 2, 1)
    homologs = jnp.broadcast_to(homologs[..., None], (2, PLANE + 1, HD // 2, 128))
    steps = jnp.concatenate([both[:, :, end : end + 4], both[:, :, end + 4 :]], 1)
    steps = steps.transpose(0, 2, 1).reshape(2, 2, 2, HD, 1)
    steps = jnp.broadcast_to(steps, (2, 2, 2, HD, VOCAB)).transpose(0, 1, 3, 2, 4)
    return column, homologs, steps.reshape(2, 2, HD, TILE)


def local(
    token_ids,
    span_offset,
    shard_lengths,
    embed_table,
    norm_gain,
    query_weight,
    key_weight,
    value_weight,
    cache_keys,
    cache_values,
):
    group = lax.axis_index("group")
    plane = lax.axis_index("yh")
    head = lax.axis_index("zx")
    mp = lax.axis_index("mp")
    tiles = jnp.where(group == 0, jnp.array(TILES[0], jnp.int32), jnp.array(TILES[1], jnp.int32))
    inside = span_offset % PROT
    where = jnp.concatenate([jnp.stack([group, plane, mp, head]).astype(jnp.int32), tiles, inside])
    swap = [(0, 1), (1, 0)]

    row = token_ids.astype(F32)
    beside = lax.ppermute(row, "yh", swap)
    upper = lax.ppermute(row, "group", [(0, 1)])
    across = lax.ppermute(row, ("group", "yh"), [(0, 3), (1, 2)])
    first = jnp.concatenate([row, beside], 1)
    prefill = jnp.where(group == 0, first, jnp.concatenate([upper, across], 1))
    size = jnp.broadcast_to(shard_lengths[None], (1, 128))
    sizes = jnp.concatenate([size // 16, size % 16], 1).astype(F32)
    small = jnp.pad(jnp.concatenate([prefill, first, sizes], 0), ((0, 5), (0, 128)))
    mine = lax.all_to_all(turn(where, small, cache_keys, cache_values), "zx", 0, 0, tiled=True)

    wide_embed = embed_table.astype(F32)
    square = jnp.sum(wide_embed * wide_embed, 1)
    square = square + lax.ppermute(square, "mp", swap)
    own, other = table(
        where,
        embed_table,
        norm_gain[None],
        square[:, None],
        query_weight,
        key_weight,
        value_weight,
    )
    recv = lax.ppermute(other, "mp", swap)
    mine = gate(mine, recv)
    peer = lax.ppermute(mine, "group", swap)
    angles = angle_tables(span_offset[0])
    query, top, acc, own_part, dec, lengths = fresh(where, own, recv, mine, *angles)
    sent, kept = cached(where, lengths, mine, peer, query, top, acc)
    got = lax.ppermute(sent, "group", [(1, 0)])
    blocks = spread(where, sent, kept, got, dec, own_part)
    parts = lax.all_to_all(blocks, ("yh", "zx"), 0, 0, tiled=True)
    return join(parts)[None]


def solution(mesh):
    inner = Mesh(mesh.devices.reshape(2, 2, PLANE, 2), ("group", "yh", "zx", "mp"))
    ctx = ("yh", "zx")
    placed = (
        P("group", ctx),
        P(),
        P(ctx),
        P(None, "mp"),
        P("mp"),
        P("mp", None),
        P("mp", None),
        P("mp", None),
        P(ctx, "mp"),
        P(ctx, "mp"),
    )
    return jax.shard_map(
        local, mesh=inner, in_specs=placed, out_specs=P("group", ctx, "mp"), check_vma=False
    )
```

time: 148 us -> 215 us (1.45)
  Pallas kernels: 71.6 us -> 135 us
  starting transfers between devices: 23.9 us -> 40.4 us
  waiting for transfers between devices: 19.7 us -> 14.2 us
  local copies, waits for them, and re-layouts: 7.43 us -> 4.44 us
  other arithmetic: 5.23 us -> 2.68 us
    pallas_call x1, Pallas kernels: 29.4 us -> 108 us  [cached(): pl.pallas_call(cached_kernel, out_shape=[jax.ShapeDtypeStruct((SENT, 96,...]
    ppermute x1, starting transfers between devices: 4.65 us -> 25.2 us  [local(): got = lax.ppermute(sent, 'group', [(1, 0)])]
    all_to_all x2 -> x1, waiting for transfers between devices: 16.1 us -> 4.79 us  [local(): lax.all_to_all(turn(where, small, cache_keys, cache_values), 'zx', 0, 0,...]
    pallas_call x1, Pallas kernels: 25.2 us -> 15.1 us  [fresh(): pl.pallas_call(fresh_kernel, out_shape=[jax.ShapeDtypeStruct((SLOTS, 256,...]
    all_to_all x2 -> x1, starting transfers between devices: 14.4 us -> 7.74 us  [local(): lax.all_to_all(turn(where, small, cache_keys, cache_values), 'zx', 0, 0,...]
    ppermute x1 -> x3, starting transfers between devices: 1.29 us -> 6.3 us  [the longest x1 3.73 us: local(): beside = lax.ppermute(row, 'yh', swap)]
    pallas_call x1, Pallas kernels: 5.95 us -> 1.98 us  [spread(): pl.pallas_call(spread_kernel, out_shape=jax.ShapeDtypeStruct((N_CTX, 96,...]
    ppermute x1 -> x3, waiting for transfers between devices: 0.01 us -> 2.36 us  [the longest x1 2.36 us: local(): across = lax.ppermute(row, ('group', 'yh'), [(0, 3), (1, 2)])]
  transfers between devices with their start and end apart: 7 -> 8, of which waited for: 4 -> 5; matrix products, arithmetic and copies ran while one was open for 6% -> 2% of each run, Pallas kernels for 23% -> 10%
where the time goes in v2:
time: 215 us; the launch traced here: 217 us
  Pallas kernels  135 us (63%)
  starting transfers between devices  40.4 us (19%)
  blocking collectives  18.6 us (9%)
  waiting for transfers between devices  14.2 us (7%)
  local copies, waits for them, and re-layouts  4.44 us (2%)
  other arithmetic  2.68 us (1%)
    pallas_call x1, Pallas kernels, cached(): pl.pallas_call(cached_kernel, out_shape=[jax.ShapeDtypeStruct((SENT, 96,...  108 us
    ppermute x1, starting transfers between devices, local(): got = lax.ppermute(sent, 'group', [(1, 0)])  25.2 us
    all_to_all x1, blocking collectives, local(): parts = lax.all_to_all(blocks, ('yh', 'zx'), 0, 0, tiled=True)  18.6 us
    pallas_call x1, Pallas kernels, fresh(): pl.pallas_call(fresh_kernel, out_shape=[jax.ShapeDtypeStruct((SLOTS, 256,...  15.1 us
    all_to_all x1, starting transfers between devices, local(): lax.all_to_all(turn(where, small, cache_keys, cache_values), 'zx', 0, 0,...  7.74 us
    pallas_call x1, Pallas kernels, table(): pl.pallas_call(table_kernel, out_shape=[jax.ShapeDtypeStruct((3 * HD, VOC...  5.77 us
    all_to_all x1, waiting for transfers between devices, local(): lax.all_to_all(turn(where, small, cache_keys, cache_values), 'zx', 0, 0,...  4.79 us
    ppermute x1, waiting for transfers between devices, local(): recv = lax.ppermute(other, 'mp', swap)  4.47 us
  transfers between devices with their start and end apart: 8, of which 5 were waited for; matrix products, arithmetic and copies ran while one was open for 2% of the time, Pallas kernels for 10%

profile of v2, /device:TPU:1, one launch (start us, length us, event | category | flops | bytes accessed | tf_op | source)
XLA Modules:
  0.0 216.8 jit_solution(15314634357654457812)
XLA Ops:
  0.0 0.7 convert_element_type.24
  0.7 3.7 %collective-permute-start.2 = (f32[1,128]{1,0:T(1,128)S(1)}, f32[1,128]{1,0:T(1,128)S(1)}, u32[]{:S(2)}, u32[]{:S(2)}) collective-permute-start(f32[1,128]{1,0:T(1,128)S(1)} %convert_element_type.24), channel_id=1, source_target_pairs={{0,32},{32,0},{1,33},{33,1},{2,34},{34,2},{3,35},{35,3},{4,36},{36... | collective-permute-start | bytes 1544 | tf_op jit(solution)/shard_map/ppermute | solution.py:721
  4.4 1.3 collective-permute-start.3
  5.7 1.3 collective-permute-start.4
  8.3 0.7 broadcast_select_fusion.1
  9.0 0.7 concatenate.45.where_ref
  9.7 0.0 collective-permute-done.2
  9.7 0.0 collective-permute-done.3
  9.7 2.4 %collective-permute-done.4 = f32[1,128]{1,0:T(1,128)S(1)} collective-permute-done((f32[1,128]{1,0:T(1,128)S(1)}, f32[1,128]{1,0:T(1,128)S(1)}, u32[]{:S(2)}, u32[]{:S(2)}) %collective-permute-start.4) | collective-permute-done | bytes 544 | tf_op jit(solution)/shard_map/ppermute | solution.py:723
  12.1 0.6 select_maximum_fusion.small_ref
  12.7 3.2 %turn.1 = bf16[16,88,384]{2,1,0:T(8,128)(2,1)} custom-call(s32[15]{0:T(128)} %concatenate.45.where_ref, f32[8,384]{1,0:T(8,128)} %select_maximum_fusion.small_ref, bf16[384,1280]{1,0:T(8,128)(2,1)} %keys_ref.1, bf16[384,1280]{1,0:T(8,128)(2,1)} %values_ref.1), custom_call_target="tpu_custom_call" | custom-call | tf_op jit(solution)/shard_map/turn/pallas_call | solution.py:94
  15.9 0.0 copy-start.6
  16.0 0.0 copy-start.7
  16.0 7.7 %all-to-all-start = ((bf16[16,88,384]{2,1,0:T(8,128)(2,1)}), bf16[16,88,384]{2,1,0:T(8,128)(2,1)S(1)}, u32[]{:S(2)}, u32[]{:S(2)}) async-start(bf16[16,88,384]{2,1,0:T(8,128)(2,1)} %turn.1), calls=%async_computation | async-start | bytes 2162688 | tf_op jit(solution)/shard_map/all_to_all | solution.py:729
  23.7 0.0 copy-done.6
  23.7 0.1 multiply_reduce_fusion
  23.9 0.5 collective-permute-start
  24.4 0.0 copy-done.7
  24.4 0.6 broadcast_in_dim.12.gain_ref
  25.0 1.4 collective-permute-done
  26.4 0.7 copy.21.square_ref
  27.1 5.8 %table.1 = (f32[240,128]{1,0:T(8,128)}, f32[240,128]{1,0:T(8,128)}) custom-call(s32[15]{0:T(128)} %concatenate.45.where_ref, bf16[128,1280]{1,0:T(8,128)(2,1)} %embed_ref.1, bf16[1,1280]{1,0:T(2,128)(2,1)} %broadcast_in_dim.12.gain_ref, f32[128,1]{1,0:T(8,128)} %copy.21.square_ref, bf16[1280,2560]{1,0:T(8,128)(2,1)} %wq.1, bf16[1280,2560]{1,0:T(8,128)(2,1)} %wk.1, ...), custom_call_target="tpu_custom_call" | custom-call | tf_op jit(solution)/shard_map/table/pallas_call | solution.py:147
  32.9 0.5 collective-permute-start.1
  33.4 4.5 %collective-permute-done.1.earlier_ref.recv_ref = f32[240,128]{1,0:T(8,128)S(1)} collective-permute-done((f32[240,128]{1,0:T(8,128)}, f32[240,128]{1,0:T(8,128)S(1)}, u32[]{:S(2)}, u32[]{:S(2)}) %collective-permute-start.1) | collective-permute-done | bytes 122912 | tf_op jit(solution)/shard_map/ppermute | solution.py:743
  37.8 0.0 copy-start.2
  37.9 4.8 %all-to-all-done.value_ref = bf16[16,88,384]{2,1,0:T(8,128)(2,1)S(1)} async-done(((bf16[16,88,384]{2,1,0:T(8,128)(2,1)}), bf16[16,88,384]{2,1,0:T(8,128)(2,1)S(1)}, u32[]{:S(2)}, u32[]{:S(2)}) %all-to-all-start) | async-done | bytes 1081376 | tf_op jit(solution)/shard_map/all_to_all | solution.py:729
  42.6 0.0 copy-done.2
  42.6 0.0 copy-start
  42.6 1.0 copy-done
  43.7 0.2 collective-permute-start.5
  43.9 0.1 mul.30
  43.9 0.1 add_convert_fusion
  44.0 0.3 multiply_sine_fusion
  44.3 0.1 fusion.1
  44.4 0.0 copy-start.1
  44.4 0.0 copy-start.3
  44.4 0.0 copy-start.4
  44.4 0.0 copy-start.5
  44.5 0.1 copy.23
  44.5 0.1 copy.24
  44.6 0.1 pad_maximum_fusion.1
  44.7 0.1 copy.25
  44.8 0.4 broadcast_bitcast_fusion
  45.2 0.3 reshape.238.step_ref
  45.5 0.1 copy.22
  45.6 0.2 broadcast_in_dim.14.homolog_ref
  45.9 0.0 copy-done.1
  45.9 0.0 copy-done.3
  45.9 0.0 copy-done.4
  45.9 0.0 copy-done.5
  45.9 15.1 %fresh.1 = (bf16[10,256,256]{2,1,0:T(8,128)(2,1)S(1)}, f32[10,1,256]{2,1,0:T(1,128)S(1)}, f32[10,96,256]{2,1,0:T(8,128)S(1)}, f32[16,88,128]{2,1,0:T(8,128)S(1)}...) custom-call(s32[15]{0:T(128)S(1)} %copy-done.5, f32[240,128]{1,0:T(8,128)S(1)} %copy-done.4, f32[240,128]{1,0:T(8,128)S(1)} %copy-done.3, ...), custom_call_target="tpu_custom_call" | custom-call | tf_op jit(solution)/shard_map/fresh/pallas_call | solution.py:399
  61.1 0.0 collective-permute-done.5.peer_ref
  61.1 107.8 %cached.1 = (bf16[6,96,256]{2,1,0:T(8,128)(2,1)S(1)}, bf16[4,96,256]{2,1,0:T(8,128)(2,1)S(1)}) custom-call(s32[15]{0:T(128)S(1)} %copy-done.5, s32[16,128]{1,0:T(8,128)S(1)} %get-tuple-element.17.length_ref, bf16[16,88,384]{2,1,0:T(8,128)(2,1)S(1)} %copy-done.1, bf16[16,88,384]{2,1,0:T(8,128)(2,1)S(1)} %collective-permute-done.5.peer_ref, ...), custom_call_target="tpu_custom_call" | custom-call | tf_op jit(solution)/shard_map/cached/pallas_call | solution.py:559
  168.9 25.2 %collective-permute-start.6 = (bf16[6,96,256]{2,1,0:T(8,128)(2,1)S(1)}, bf16[6,96,256]{2,1,0:T(8,128)(2,1)S(1)}, u32[]{:S(2)}, u32[]{:S(2)}) collective-permute-start(bf16[6,96,256]{2,1,0:T(8,128)(2,1)S(1)} %get-tuple-element.21.sent_ref), channel_id=1, source_target_pairs={{64,0},{65,1},{66,2},{67,3},{68,4},{69,5},{70,6},{71,7},{72,8},{73... | collective-permute-start | bytes 884744 | tf_op jit(solution)/shard_map/ppermute | solution.py:749
  194.1 1.2 collective-permute-done.6.got_ref
  195.3 2.0 spread.1
  197.3 18.6 %all_to_all.10.parts_ref = bf16[32,96,128]{2,1,0:T(8,128)(2,1)S(1)} all-to-all(bf16[32,96,128]{2,1,0:T(8,128)(2,1)S(1)} %spread.1), channel_id=1, replica_groups=mesh['group'=2,'yh'=2,'zx'=16,'mp'=2] {'yh','zx'}, dimensions={0} | all-to-all | bytes 1572864 | tf_op jit(solution)/shard_map/all_to_all | solution.py:751
  215.9 1.0 join.1
  (12 shorter events, 0.1 us)
Async XLA Ops:
  0.7 9.1 %collective-permute-start.2 = (f32[1,128]{1,0:T(1,128)S(1)}, f32[1,128]{1,0:T(1,128)S(1)}, u32[]{:S(2)}, u32[]{:S(2)}) collective-permute-start(f32[1,128]{1,0:T(1,128)S(1)} %convert_element_type.24), channel_id=1, source_target_pairs={{0,32},{32,0},{1,33},{33,1},{2,34},{34,2},{3,35},{35,3},{4,36},{36... | collective-permute-start | bytes 1544 | tf_op jit(solution)/shard_map/ppermute | solution.py:721
  4.4 5.3 %collective-permute-start.3 = (f32[1,128]{1,0:T(1,128)S(1)}, f32[1,128]{1,0:T(1,128)S(1)}, u32[]{:S(2)}, u32[]{:S(2)}) collective-permute-start(f32[1,128]{1,0:T(1,128)S(1)} %convert_element_type.24), channel_id=1, source_target_pairs={{0,64},{1,65},{2,66},{3,67},{4,68},{5,69},{6,70},{7,71},{8,72},{9,... | collective-permute-start | bytes 1544 | tf_op jit(solution)/shard_map/ppermute | solution.py:722
  5.7 6.4 %collective-permute-start.4 = (f32[1,128]{1,0:T(1,128)S(1)}, f32[1,128]{1,0:T(1,128)S(1)}, u32[]{:S(2)}, u32[]{:S(2)}) collective-permute-start(f32[1,128]{1,0:T(1,128)S(1)} %convert_element_type.24), channel_id=1, source_target_pairs={{0,96},{32,64},{1,97},{33,65},{2,98},{34,66},{3,99},{35,67},{4,100... | collective-permute-start | bytes 1544 | tf_op jit(solution)/shard_map/ppermute | solution.py:723
  15.9 7.8 %copy-start.6 = (bf16[128,1280]{1,0:T(8,128)(2,1)S(1)}, bf16[128,1280]{1,0:T(8,128)(2,1)}, u32[]{:S(2)}) copy-start(bf16[128,1280]{1,0:T(8,128)(2,1)} %embed_ref.1) | copy-start | bytes 983044
  16.0 8.4 %copy-start.7 = (bf16[1280]{0:T(1024)(128)(2,1)S(1)}, bf16[1280]{0:T(1024)(128)(2,1)}, u32[]{:S(2)}) copy-start(bf16[1280]{0:T(1024)(128)(2,1)} %param.16) | copy-start | bytes 7684
  16.0 26.7 %all-to-all-start = ((bf16[16,88,384]{2,1,0:T(8,128)(2,1)}), bf16[16,88,384]{2,1,0:T(8,128)(2,1)S(1)}, u32[]{:S(2)}, u32[]{:S(2)}) async-start(bf16[16,88,384]{2,1,0:T(8,128)(2,1)} %turn.1), calls=%async_computation | async-start | bytes 2162688 | tf_op jit(solution)/shard_map/all_to_all | solution.py:729
  23.9 2.5 %collective-permute-start = (f32[128]{0:T(128)S(1)}, f32[128]{0:T(128)S(1)}, u32[]{:S(2)}, u32[]{:S(2)}) collective-permute-start(f32[128]{0:T(128)S(1)} %multiply_reduce_fusion), channel_id=1, source_target_pairs={{0,1},{1,0},{2,3},{3,2},{4,5},{5,4},{6,7},{7,6},{8,9},{9,8},{10,11... | collective-permute-start | bytes 1544 | tf_op jit(solution)/shard_map/ppermute | solution.py:733
  32.9 5.0 %collective-permute-start.1 = (f32[240,128]{1,0:T(8,128)}, f32[240,128]{1,0:T(8,128)S(1)}, u32[]{:S(2)}, u32[]{:S(2)}) collective-permute-start(f32[240,128]{1,0:T(8,128)} %get-tuple-element.16), channel_id=1, source_target_pairs={{0,1},{1,0},{2,3},{3,2},{4,5},{5,4},{6,7},{7,6},{8,9},{9,8},{10,11... | collective-permute-start | bytes 368648 | tf_op jit(solution)/shard_map/ppermute | solution.py:743
  37.8 4.8 %copy-start.2 = (f32[240,128]{1,0:T(8,128)}, f32[240,128]{1,0:T(8,128)S(1)}, u32[]{:S(2)}) copy-start(f32[240,128]{1,0:T(8,128)S(1)} %collective-permute-done.1.earlier_ref.recv_ref) | copy-start | bytes 368644
  42.6 1.0 copy-start
  43.7 17.4 %collective-permute-start.5 = (bf16[16,88,384]{2,1,0:T(8,128)(2,1)}, bf16[16,88,384]{2,1,0:T(8,128)(2,1)S(1)}, u32[]{:S(2)}, u32[]{:S(2)}) collective-permute-start(bf16[16,88,384]{2,1,0:T(8,128)(2,1)} %gate.1.mine_ref), channel_id=1, source_target_pairs={{0,64},{64,0},{1,65},{65,1},{2,66},{66,2},{3,67},{67,3},{4,68},{68... | collective-permute-start | bytes 3244040 | tf_op jit(solution)/shard_map/ppermute | solution.py:745
  44.4 1.5 copy-start.1
  44.4 1.5 copy-start.3
  44.4 1.5 copy-start.4
  44.4 1.5 copy-start.5
  168.9 26.4 %collective-permute-start.6 = (bf16[6,96,256]{2,1,0:T(8,128)(2,1)S(1)}, bf16[6,96,256]{2,1,0:T(8,128)(2,1)S(1)}, u32[]{:S(2)}, u32[]{:S(2)}) collective-permute-start(bf16[6,96,256]{2,1,0:T(8,128)(2,1)S(1)} %get-tuple-element.21.sent_ref), channel_id=1, source_target_pairs={{64,0},{65,1},{66,2},{67,3},{68,4},{69,5},{70,6},{71,7},{72,8},{73... | collective-permute-start | bytes 884744 | tf_op jit(solution)/shard_map/ppermute | solution.py:749
